TPU v7x, 32 devices: a whole 2x2x4 slice. The times are simulated.
32 devices in a mesh: var: 8 (over z, core), samp: 4 (over y, x).
Axes of the slice: x: 2, y: 2, z: 4, core: 2. Of those that a mesh axis runs over, the one named last changes fastest.
Arguments:
- geno: bfloat16 [8192, 16384], P('samp', 'var'), may hold values from -5 to 5
- scale_index: int32 [64, 16384], P('samp', 'var'), may hold values from 0 to 15
- scale_table: float32 [16], replicated, may hold values from 0.25 to 4
- residual: float32 [8, 8192], P(None, 'samp'), may hold values from -6 to 6
- beta_active: float32 [8, 3584], P(None, 'var'), may hold values from -6 to 6
- block_inverse: float32 [16, 256, 256], P('var'), may hold values from -1 to 4
- active_ids: int32 [3584], P('var'), may hold values from 0 to 16383, as said below
- admit_ids: int32 [512], P('var'), may hold values from 0 to 16383, as said below
Outputs:
- scores: float32 [8, 16384], P(None, 'var')
- coefficients: float32 [8, 4096], P(None, 'var')
- residual_out: float32 [8, 8192], P(None, 'samp')
Inputs may be any that keep to these rules, and one draw needn't show every extreme that they name: Variant ids, all different from one another and from those of admit_ids. The fitting slots of one index of var are its 448 entries of active_ids followed by its 64 entries of admit_ids; of these 512 slots at most 128 name variants held by any one index of var, and for every index of var some one holder reaches exactly 128. `admit_ids`: variant ids, as for active_ids.
All inputs are finite; a program needn't handle non-finite values.
Results may differ from a plain program's by a relative error of at most 0.004.
Values may be sent and summed in bfloat16 or wider, within the bound.
A program may use at most 128 MiB of HBM per device.

v0:
```python
import functools
import math

import jax
import jax.numpy as jnp
from jax import lax
from jax.experimental import pallas as pl
from jax.experimental.pallas import tpu as pltpu
from jax.sharding import PartitionSpec as P

PASSES = 3
PENALTY = 0.5
EPSILON = 1e-06
LANES = 128
F32 = jnp.float32
BF16 = jnp.bfloat16
NN = (((1,), (0,)), ((), ()))
NT = (((1,), (1,)), ((), ()))


def dot(a, b, dims=NN):
    return lax.dot_general(a, b, dims, preferred_element_type=F32)


def split(x):
    high = x.astype(BF16).astype(F32)
    return jnp.concatenate([high, x - high], axis=0).astype(BF16)


def joined(x):
    half = x.shape[0] // 2
    return x[:half] + x[half:]


def kernel(
    V, S, pad,
    geno, sidx, table, resid, beta, binv, active, admit,
    scores_out, coef_out, resid_out,
    x_ref, scale_ref, rlow, part, pick, unpick, tri, inv_hi, inv_lo, ids_all, src_row,
    packed, d_got, d_held, up_two, coef, grad, direct,
    send_a, recv_a, send_b, recv_b, send_c, recv_c, recv_u, recv_p, recv_s,
    load_sem, send_sem, recv_sem,
):
    N = V * S
    rows, width = x_ref.shape
    groups = sidx.shape[0]
    per_group = rows // groups
    levels = table.shape[0]
    ph = resid.shape[0]
    kept = active.shape[1]
    fit = kept + admit.shape[1]
    blocks, bsize = binv.shape[0], binv.shape[1]
    chunk = rows // V
    step = 2 * per_group
    n_steps = rows // step
    inv_root = 1.0 / math.sqrt(rows * S)
    mv, ms = lax.axis_index("var"), lax.axis_index("samp")
    me = ms * V + mv

    def load(i):
        at = pl.ds(pl.multiple_of(i * step, step), step)
        return pltpu.make_async_copy(geno.at[at], x_ref.at[at], load_sem.at[i])

    for i in range(n_steps):
        load(i).start()

    barrier = pltpu.get_barrier_semaphore()

    def other(k):
        t = lax.rem(me + k, N)
        return lax.div(t, V), lax.rem(t, V)

    def greet(k, c):
        s, v = other(k)
        pl.semaphore_signal(
            barrier, inc=1, device_id={"var": v, "samp": s}, device_id_type=pl.DeviceIdType.MESH
        )
        return c

    lax.fori_loop(1, N, greet, 0)

    def send(src, dst, sem, v, s):
        pltpu.make_async_remote_copy(
            src_ref=src, dst_ref=dst, send_sem=send_sem.at[sem], recv_sem=recv_sem.at[sem],
            device_id={"var": v, "samp": s}, device_id_type=pl.DeviceIdType.MESH,
        ).start()

    def got(ref, sem):
        pltpu.make_async_copy(ref, ref, recv_sem.at[sem]).wait()

    def sent(ref, sem):
        pltpu.make_async_copy(ref, ref, send_sem.at[sem]).wait()

    def var_peers(fn):
        def one(k, c):
            fn(lax.rem(mv + k, V))
            return c

        lax.fori_loop(1, V, one, 0)

    IDS, A, B, C, U, SC, SM = 0, 1, 1 + PASSES, 1 + 2 * PASSES, 1 + 3 * PASSES, 1 + 4 * PASSES, 2 + 4 * PASSES

    ids_all[mv, :, 0:kept] = jnp.broadcast_to(active[...], (8, kept))
    ids_all[mv, :, kept:fit] = jnp.broadcast_to(admit[...], (8, fit - kept))
    index = sidx[...]
    scales = jnp.zeros(index.shape, F32)
    for level in range(levels):
        scales = jnp.where(index == level, table[level], scales)
    scale_ref[...] = scales
    rlow[...] = resid[...].astype(BF16)
    for b in range(blocks):
        whole = binv[b]
        high = whole.astype(BF16)
        inv_hi[b] = high
        inv_lo[b] = (whole - high.astype(F32)).astype(BF16)
    coef[...] = jnp.zeros((ph, fit), F32)
    coef[:, 0:kept] = beta[...]
    tri[...] = jnp.where(
        lax.broadcasted_iota(jnp.int32, (fit, fit), 0) < lax.broadcasted_iota(jnp.int32, (fit, fit), 1),
        1.0, 0.0,
    ).astype(BF16)

    pl.semaphore_wait(barrier, N - 1)
    var_peers(lambda v: send(ids_all.at[mv], ids_all.at[mv], IDS, v, ms))

    part[...] = jnp.zeros((ph, width), F32)
    cols = 512

    def screen(i, c):
        load(i).wait()
        for half in range(2):
            at = pl.ds(pl.multiple_of(i * step + half * per_group, per_group), per_group)
            for j in range(width // cols):
                lane = slice(j * cols, (j + 1) * cols)
                scale = scale_ref[pl.ds(2 * i + half, 1), lane]
                x_ref[at, lane] = (x_ref[at, lane].astype(F32) * scale).astype(BF16)
        at = pl.ds(pl.multiple_of(i * step, step), step)
        part[...] += dot(rlow[:, at], x_ref[at, :])
        return c

    lax.fori_loop(0, n_steps, screen, 0)
    recv_p[ms] = part[...]

    got(ids_all.at[pl.ds(0, V - 1)], IDS)
    line = lax.broadcasted_iota(jnp.int32, (V, fit), 0)
    all_ids = jnp.zeros((V, fit), jnp.int32)
    for g in range(V):
        all_ids = jnp.where(line == g, ids_all[g][0:1], all_ids)
    column = all_ids - mv * width
    held = (column >= 0) & (column < width)
    serial = dot(jnp.where(held, 1.0, 0.0).astype(BF16), tri[...]).astype(jnp.int32)
    serial = jnp.where(held, serial, -1)
    column = jnp.where(held, column, 0)
    eight = lax.broadcasted_iota(jnp.int32, (8, fit), 0)
    turn = lax.broadcasted_iota(jnp.int32, (pad, fit), 0)
    for g in range(V):
        col = column[g:g + 1]
        digits = jnp.where(
            eight == 0, lax.shift_right_logical(col, 7),
            jnp.where(eight == 1, col & 127, jnp.where(eight == 2, 1, 0)),
        ).astype(F32).astype(BF16)
        place = jnp.where(turn == serial[g:g + 1], 1.0, 0.0).astype(BF16)
        found = dot(digits, place, NT)
        where = jnp.where(found[2:3] > 0.5, found[0:1] * 128.0 + found[1:2], -1.0)
        src_row[g] = jnp.broadcast_to(where.astype(jnp.int32), (8, pad))

    def mark(i, c):
        at = pl.ds(pl.multiple_of(i * 256, 256), 256)
        here = lax.broadcasted_iota(jnp.int32, (256, pad), 0) + i * 256
        for g in range(V):
            pick[at, g * pad:(g + 1) * pad] = jnp.where(here == src_row[g][0:1], 1.0, 0.0).astype(BF16)
        return c

    lax.fori_loop(0, width // 256, mark, 0)

    mine = ids_all[mv][0:1] - line * width
    marks = jnp.where((mine >= 0) & (mine < width), 1.0, 0.0)
    before = dot(marks.astype(BF16), tri[...])
    position = jnp.sum(marks * (before + line.astype(F32) * float(pad)), axis=0, keepdims=True)
    position = position.astype(jnp.int32)

    def place_own(i, c):
        at = pl.ds(pl.multiple_of(i * 128, 128), 128)
        here = lax.broadcasted_iota(jnp.int32, (128, fit), 0) + i * 128
        unpick[at, :] = jnp.where(here == position, 1.0, 0.0).astype(BF16)
        return c

    lax.fori_loop(0, V * pad // 128, place_own, 0)

    resid_out[...] = resid[...]
    lane = lax.broadcasted_iota(jnp.int32, (ph, LANES), 1)

    def length(p):
        got(recv_s.at[p, pl.ds(0, S - 1)], SM + p)
        total = recv_s[p, 0]
        for s in range(1, S):
            total = total + recv_s[p, s]
        return total[:, 0:1] / (total[:, 1:2] + EPSILON)

    def tell_sums(p):
        cross = jnp.zeros((ph, chunk), F32)
        square = jnp.zeros((ph, chunk), F32)
        for v in range(V):
            upd = recv_u[p, v]
            cross = cross + resid_out[:, v * chunk:(v + 1) * chunk] * upd
            square = square + upd * upd
        cross = jnp.sum(cross, axis=1, keepdims=True)
        square = jnp.sum(square, axis=1, keepdims=True)
        recv_s[p, ms] = jnp.where(lane == 0, cross, jnp.where(lane == 1, square, 0.0))

        def tell(k, c):
            send(recv_s.at[p, ms], recv_s.at[p, ms], SM + p, mv, lax.rem(ms + k, S))
            return c

        lax.fori_loop(1, S, tell, 0)

    def advance(factor, p):
        for v in range(V):
            at = slice(v * chunk, (v + 1) * chunk)
            resid_out[:, at] = resid_out[:, at] - factor * recv_u[p, v]

    for p in range(PASSES):
        up_two[...] = split(part[...])
        wide = 2 * pad

        for n in range(V * pad // wide):
            out = joined(dot(up_two[...], pick[:, n * wide:(n + 1) * wide]))
            for q in range(2):
                send_a[p, 2 * n + q] = out[:, q * pad:(q + 1) * pad].astype(BF16)

        def route(k, c):
            s, v = other(k)
            send(send_a.at[p, v], recv_a.at[p, me], A + p, v, s)
            return c

        lax.fori_loop(1, N, route, 0)
        recv_a[p, me] = send_a[p, mv]
        if p == 0:
            def share(k, c):
                send(recv_p.at[ms], recv_p.at[ms], SC, mv, lax.rem(ms + k, S))
                return c

            lax.fori_loop(1, S, share, 0)
        got(recv_a.at[p, pl.ds(0, N - 1)], A + p)
        for v in range(V):
            val = recv_a[p, v].astype(F32)
            for s in range(1, S):
                val = val + recv_a[p, s * V + v].astype(F32)
            packed[:, v * pad:(v + 1) * pad] = split(val)
        slots = joined(dot(packed[...], unpick[...])) * inv_root
        if p == 0:
            grad[...] = slots
        else:
            factor = length(p - 1)
            grad[...] = grad[...] - factor * slots
            coef[...] = coef[...] + factor * direct[...].astype(F32)
        inner = grad[...] - PENALTY * coef[...]
        for b in range(blocks):
            at = slice(b * bsize, (b + 1) * bsize)
            two = split(inner[:, at])
            main = joined(dot(two, inv_hi[b], NT))
            rest = dot(two, inv_lo[b], NT)
            direct[:, at] = (main + rest[:ph]).astype(BF16)

        back = dot(direct[...], unpick[...], NT)
        for v in range(V):
            send_b[p, v] = back[:, v * pad:(v + 1) * pad].astype(BF16)
        var_peers(lambda v: send(send_b.at[p, v], recv_b.at[p, mv], B + p, v, ms))
        recv_b[p, mv] = send_b[p, mv]
        if p > 0:
            advance(factor, p - 1)
        got(recv_b.at[p, pl.ds(0, V - 1)], B + p)
        for v in range(V):
            d_got[:, v * pad:(v + 1) * pad] = recv_b[p, v]
        def spread(i, c):
            at = pl.ds(pl.multiple_of(i * 512, 512), 512)
            d_held[:, at] = dot(d_got[...], pick[at, :], NT).astype(BF16)
            return c

        lax.fori_loop(0, width // 512, spread, 0)

        def piece(v):
            at = pl.ds(pl.multiple_of(v * chunk, chunk), chunk)
            return dot(d_held[...], x_ref[at, :], NT)

        def give(v):
            send_c[p, v] = piece(v).astype(BF16)
            send(send_c.at[p, v], recv_c.at[p, mv], C + p, v, ms)

        var_peers(give)
        recv_c[p, mv] = piece(mv).astype(BF16)
        got(recv_c.at[p, pl.ds(0, V - 1)], C + p)
        val = recv_c[p, 0].astype(F32)
        for v in range(1, V):
            val = val + recv_c[p, v].astype(F32)
        val = val * inv_root
        recv_u[p, mv] = val
        var_peers(lambda v: send(recv_u.at[p, mv], recv_u.at[p, mv], U + p, v, ms))
        got(recv_u.at[p, pl.ds(0, V - 1)], U + p)
        tell_sums(p)
        if p + 1 < PASSES:
            for v in range(V):
                up_two[:, v * chunk:(v + 1) * chunk] = split(recv_u[p, v])

            def project(i, c):
                at = pl.ds(pl.multiple_of(i * 256, 256), 256)
                part[:, at] = joined(dot(up_two[...], x_ref[:, at]))
                return c

            lax.fori_loop(0, width // 256, project, 0)

    got(recv_p.at[pl.ds(0, S - 1)], SC)
    val = recv_p[0]
    for s in range(1, S):
        val = val + recv_p[s]
    scores_out[...] = val * inv_root
    factor = length(PASSES - 1)
    advance(factor, PASSES - 1)
    coef_out[...] = coef[...] + factor * direct[...].astype(F32)

    sent(ids_all.at[pl.ds(0, V - 1)], IDS)
    sent(recv_p.at[pl.ds(0, S - 1)], SC)
    for p in range(PASSES):
        sent(recv_a.at[p, pl.ds(0, N - 1)], A + p)
        sent(recv_s.at[p, pl.ds(0, S - 1)], SM + p)
        sent(recv_b.at[p, pl.ds(0, V - 1)], B + p)
        sent(recv_c.at[p, pl.ds(0, V - 1)], C + p)
        sent(recv_u.at[p, pl.ds(0, V - 1)], U + p)


def on_device(geno, scale_index, scale_table, residual, beta_active, block_inverse, active_ids, admit_ids):
    V, S = lax.axis_size("var"), lax.axis_size("samp")
    N = V * S
    rows, width = geno.shape
    ph = residual.shape[0]
    fit = active_ids.shape[0] + admit_ids.shape[0]
    pad = LANES * pl.cdiv(2 * fit // V, LANES)
    chunk = rows // V
    vmem = pl.BlockSpec(memory_space=pltpu.VMEM)
    n_sem = 2 + 5 * PASSES
    return pl.pallas_call(
        functools.partial(kernel, V, S, pad),
        out_shape=(
            jax.ShapeDtypeStruct((ph, width), F32),
            jax.ShapeDtypeStruct((ph, fit), F32),
            jax.ShapeDtypeStruct((ph, rows), F32),
        ),
        in_specs=[
            pl.BlockSpec(memory_space=pl.ANY), vmem, pl.BlockSpec(memory_space=pltpu.SMEM),
            vmem, vmem, vmem, vmem, vmem,
        ],
        out_specs=(vmem, vmem, vmem),
        scratch_shapes=[
            pltpu.VMEM((rows, width), BF16),
            pltpu.VMEM(scale_index.shape, F32),
            pltpu.VMEM((ph, rows), BF16),
            pltpu.VMEM((ph, width), F32),
            pltpu.VMEM((width, V * pad), BF16),
            pltpu.VMEM((V * pad, fit), BF16),
            pltpu.VMEM((fit, fit), BF16),
            pltpu.VMEM(block_inverse.shape, BF16),
            pltpu.VMEM(block_inverse.shape, BF16),
            pltpu.VMEM((V, 8, fit), jnp.int32),
            pltpu.VMEM((V, 8, pad), jnp.int32),
            pltpu.VMEM((2 * ph, V * pad), BF16),
            pltpu.VMEM((ph, V * pad), BF16),
            pltpu.VMEM((ph, width), BF16),
            pltpu.VMEM((2 * ph, width), BF16),
            pltpu.VMEM((ph, fit), F32),
            pltpu.VMEM((ph, fit), F32),
            pltpu.VMEM((ph, fit), BF16),
            pltpu.VMEM((PASSES, V, ph, pad), BF16),
            pltpu.VMEM((PASSES, N, ph, pad), BF16),
            pltpu.VMEM((PASSES, V, ph, pad), BF16),
            pltpu.VMEM((PASSES, V, ph, pad), BF16),
            pltpu.VMEM((PASSES, V, ph, chunk), BF16),
            pltpu.VMEM((PASSES, V, ph, chunk), BF16),
            pltpu.VMEM((PASSES, V, ph, chunk), F32),
            pltpu.VMEM((S, ph, width), F32),
            pltpu.VMEM((PASSES, S, ph, LANES), F32),
            pltpu.SemaphoreType.DMA((rows // (2 * (rows // scale_index.shape[0])),)),
            pltpu.SemaphoreType.DMA((n_sem,)),
            pltpu.SemaphoreType.DMA((n_sem,)),
        ],
        compiler_params=pltpu.CompilerParams(
            collective_id=0, has_side_effects=True, vmem_limit_bytes=60 * 1024 * 1024
        ),
    )(geno, scale_index, scale_table, residual, beta_active, block_inverse, active_ids[None], admit_ids[None])


def solution(mesh):
    placed = (
        P("samp", "var"), P("samp", "var"), P(), P(None, "samp"), P(None, "var"),
        P("var", None, None), P("var"), P("var"),
    )
    return jax.shard_map(
        on_device, mesh=mesh, in_specs=placed,
        out_specs=(P(None, "var"), P(None, "var"), P(None, "samp")), check_vma=False,
    )
```

profile of v0, /device:TPU:0, one launch (start us, length us, event | category | flops | bytes accessed | tf_op | source)
XLA Modules:
  0.0 89.7 jit_solution(2442704529966290641)
XLA Ops:
  0.6 84.8 %shard_map.103 = (f32[8,2048]{1,0:T(8,128)}, f32[8,512]{1,0:T(8,128)}, f32[8,2048]{1,0:T(8,128)}) custom-call(bf16[2048,2048]{1,0:T(8,128)(2,1)} %geno.1, s32[16,2048]{1,0:T(8,128)} %sidx.1, f32[16]{0:T(128)} %table.1, f32[8,2048]{1,0:T(8,128)} %resid.1, f32[8,448]{1,0:T(8,128)} %beta.1, f32[2,256,256]{2,1,0:T(8,128)} %binv.1, s32[1,448]{1,0:T(1,128)} %bitcast.2, ...), custom_call_target="tpu_custom_call" | custom-call | tf_op jit(solution)/shard_map/pallas_call | solution.py:341
  85.5 1.5 %copy.14 = f32[8,2048]{1,0:T(8,128)} copy(f32[8,2048]{1,0:T(8,128)} %get-tuple-element.6) | data formatting | bytes 131072
  87.0 1.3 %copy.15 = f32[8,512]{1,0:T(8,128)} copy(f32[8,512]{1,0:T(8,128)} %get-tuple-element.7) | data formatting | bytes 32768
  88.3 1.5 %copy.16 = f32[8,2048]{1,0:T(8,128)} copy(f32[8,2048]{1,0:T(8,128)} %get-tuple-element.8) | data formatting | bytes 131072
where the time goes:
time: 90 us; the launch traced here: 89.7 us
  Pallas kernels  84.8 us (94%)
  local copies, waits for them, and re-layouts  4.27 us (5%)
    pallas_call x1, Pallas kernels, on_device(): pl.pallas_call(functools.partial(kernel, V, S, pad), out_shape=(jax.Shape...  84.8 us
    unnamed x3, local copies, waits for them, and re-layouts  4.27 us

commit v1 on v0

v1 whole, which is shorter than its diff:
```python
import functools
import math

import jax
import jax.numpy as jnp
from jax import lax
from jax.experimental import pallas as pl
from jax.experimental.pallas import tpu as pltpu
from jax.sharding import PartitionSpec as P

PASSES = 3
PENALTY = 0.5
EPSILON = 1e-06
LANES = 128
F32 = jnp.float32
BF16 = jnp.bfloat16
NN = (((1,), (0,)), ((), ()))
NT = (((1,), (1,)), ((), ()))


def dot(a, b, dims=NN):
    return lax.dot_general(a, b, dims, preferred_element_type=F32)


def split(x):
    high = x.astype(BF16).astype(F32)
    return jnp.concatenate([high, x - high], axis=0).astype(BF16)


def joined(x):
    half = x.shape[0] // 2
    return x[:half] + x[half:]


def owners_of(V):
    return (V // 2, 2) if V % 8 == 0 else (V, 1)


def group_order(V):
    O, G = owners_of(V)
    if G == 1:
        return list(range(V))
    order = []
    for q in range(O):
        h, zc, c = q // 4, 1 + (q % 4) // 2, q % 2
        edge = 0 if zc == 1 else 3
        order += [8 * h + 2 * zc + c, 8 * h + 2 * edge + c]
    return order


def kernel(
    V, S, pad,
    geno, sidx, table, resid, beta, binv, active, admit,
    scores_out, coef_out, resid_out,
    x_ref, sidx_v, table_s, cur, beta_v, binv_v, act_v, adm_v,
    scale_ref, rlow, part, low, high_t, marks_v, place_v, tri, inv, beta_two, ids_all,
    d_held, coef, grad, direct,
    send_a, recv_a, send_b, recv_b, send_c, recv_c, recv_u, recv_p, recv_s, recv_d,
    load_sem, in_sem, send_sem, recv_sem,
):
    cur_scope = [None]

    def mk(name):
        pass

    N = V * S
    O, G = owners_of(V)
    order = group_order(V)
    rows, width = x_ref.shape
    groups = sidx_v.shape[0]
    per_group = rows // groups
    levels = table_s.shape[0]
    ph = cur.shape[0]
    kept = act_v.shape[1]
    fit = kept + adm_v.shape[1]
    blocks, bsize = binv_v.shape[0], binv_v.shape[1]
    chunk = rows // O
    tiles = width // LANES
    step = 2 * per_group
    n_steps = rows // step
    inv_root = 1.0 / math.sqrt(rows * S)
    mv, ms = lax.axis_index("var"), lax.axis_index("samp")
    me = ms * V + mv

    mk("greet")
    barrier = pltpu.get_barrier_semaphore()

    def greet(k, c):
        t = lax.rem(me + k, N)
        pl.semaphore_signal(
            barrier, inc=1, device_id={"var": lax.rem(t, V), "samp": lax.div(t, V)},
            device_id_type=pl.DeviceIdType.MESH,
        )
        return c

    lax.fori_loop(1, N, greet, 0)
    mk("start")

    def load(i):
        at = pl.ds(pl.multiple_of(i * step, step), step)
        return pltpu.make_async_copy(geno.at[at], x_ref.at[at], load_sem.at[i])

    small = [(table, table_s), (sidx, sidx_v), (resid, cur), (active, act_v), (admit, adm_v), (beta, beta_v), (binv, binv_v)]
    pulls = [pltpu.make_async_copy(a, b, in_sem.at[i]) for i, (a, b) in enumerate(small)]
    for c in pulls[:5]:
        c.start()
    load(0).start()
    load(1).start()
    for c in pulls[5:]:
        c.start()
    for i in range(2, n_steps):
        load(i).start()

    if G == 1:
        is_owner, my_q = None, mv
        owners = [(lax.rem(mv + 1 + k, V), lax.rem(mv + 1 + k, V)) for k in range(V)]
        all_var = [lax.rem(mv + 1 + k, V) for k in range(V - 1)]
        partner = None
    else:
        H = V // 8
        h, z, c0 = lax.div(mv, 8), lax.rem(lax.div(mv, 2), 4), lax.rem(mv, 2)
        side = lax.div(z, 2)
        cores = (1 - c0, c0)
        hs = [lax.rem(h + d, H) for d in range(1, H)] + [h]
        owners = [
            (8 * hh + 2 * zc + cc, 4 * hh + 2 * (zc - 1) + cc)
            for hh in hs for zc in (2 - side, 1 + side) for cc in cores
        ]
        is_owner = z == 1 + side
        my_q = 4 * h + 2 * side + c0
        z0 = z + side * (3 - 2 * z)
        zs = [side * 3 + (1 - 2 * side) * k for k in (3, 2, 1 - z0, z0)]
        all_var = [8 * hh + 2 * zz + cc for hh in hs for zz in zs for cc in cores][:-1]
        partner = 8 * h + 2 * (side * 3 + (1 - 2 * side) * (1 - z0)) + c0
    samps = [lax.rem(ms + d, S) for d in range(1, S)]

    def owner_only(fn):
        if G == 1:
            fn()
        else:
            pl.when(is_owner)(fn)

    def other_only(fn):
        if G > 1:
            pl.when(jnp.logical_not(is_owner))(fn)

    def send(src, dst, sem, v, s, r_sem=None):
        pltpu.make_async_remote_copy(
            src_ref=src, dst_ref=dst, send_sem=send_sem.at[sem],
            recv_sem=recv_sem.at[sem if r_sem is None else r_sem],
            device_id={"var": v, "samp": s}, device_id_type=pl.DeviceIdType.MESH,
        ).start()

    def got(ref, sem):
        pltpu.make_async_copy(ref, ref, recv_sem.at[sem]).wait()

    def sent(ref, sem):
        pltpu.make_async_copy(ref, ref, send_sem.at[sem]).wait()

    IDS, INV, BETA, SC = 0, 1, 2, 3
    A = 4
    B = A + PASSES
    C = B + PASSES
    SM = C + PASSES
    D = SM + PASSES
    U = D + PASSES
    UQ = U + PASSES

    mk("setup")
    for c in pulls[:5]:
        c.wait()
    ids_all[mv, :, 0:kept] = act_v[...]
    ids_all[mv, :, kept:fit] = adm_v[...]
    index = sidx_v[...]
    scales = jnp.zeros(index.shape, F32)
    for level in range(levels):
        scales = jnp.where(index == level, table_s[level], scales)
    scale_ref[...] = scales
    rlow[...] = cur[...].astype(BF16)
    part[...] = jnp.zeros((ph, width), F32)
    cols = 256

    def screen(i, c):
        load(i).wait()
        at = pl.ds(pl.multiple_of(i * step, step), step)
        left = rlow[:, at]
        for j in range(width // cols):
            lane = slice(j * cols, (j + 1) * cols)
            block = []
            for half in range(2):
                sub = pl.ds(pl.multiple_of(i * step + half * per_group, per_group), per_group)
                block.append(x_ref[sub, lane].astype(F32) * scale_ref[pl.ds(2 * i + half, 1), lane])
            block = jnp.concatenate(block, axis=0).astype(BF16)
            x_ref[at, lane] = block
            part[:, lane] += dot(left, block)
        return c

    first = (n_steps * 5) // 8
    mk("screen1")
    lax.fori_loop(0, first, screen, 0)
    mk("inv")
    for c in pulls[5:]:
        c.wait()
    for b in range(blocks):
        inv[0, b] = binv_v[b].astype(BF16)
    tri[...] = jnp.where(
        lax.broadcasted_iota(jnp.int32, (fit, fit), 0) < lax.broadcasted_iota(jnp.int32, (fit, fit), 1),
        1.0, 0.0,
    ).astype(BF16)
    mk("barrier")
    pl.semaphore_wait(barrier, N - 1)
    for v in all_var:
        send(ids_all.at[mv], ids_all.at[mv], IDS, v, ms)

    def hand_over():
        send(beta_v, beta_two, BETA, partner, ms)
        send(inv.at[0], inv.at[1], INV, partner, ms)

    other_only(hand_over)
    mk("screen2")
    lax.fori_loop(first, n_steps, screen, 0)
    recv_p[ms] = part[...]

    mk("idswait")
    got(ids_all.at[pl.ds(0, V - 1)], IDS)
    mk("idsproc")
    line = lax.broadcasted_iota(jnp.int32, (V, fit), 0)

    def lines(g):
        return ids_all[g, 0:1, :]

    all_ids = jnp.zeros((V, fit), jnp.int32)
    for g in range(V):
        all_ids = jnp.where(line == g, lines(g), all_ids)
    column = all_ids - mv * width
    held = (column >= 0) & (column < width)
    serial = dot(jnp.where(held, 1.0, 0.0).astype(BF16), tri[...])
    serial = jnp.where(held, serial, -1.0)
    column = jnp.where(held, column, 0)
    eight = lax.broadcasted_iota(jnp.int32, (8, fit), 0)
    turn = lax.broadcasted_iota(jnp.int32, (pad, fit), 0).astype(F32)
    lane_no = lax.broadcasted_iota(jnp.int32, (LANES, pad), 0).astype(F32)
    for n, g in enumerate(order):
        col = column[g:g + 1]
        digits = jnp.where(
            eight == 0, lax.shift_right_logical(col, 7),
            jnp.where(eight == 1, col & 127, jnp.where(eight == 2, 1, 0)),
        ).astype(F32).astype(BF16)
        place = jnp.where(turn == serial[g:g + 1], 1.0, 0.0).astype(BF16)
        found = dot(digits, place, NT)
        here = found[2:3] > 0.5
        at = slice(n * pad, (n + 1) * pad)
        high_t[:, at] = jnp.broadcast_to(jnp.where(here, found[0:1], -1.0), (ph, pad))
        low[:, at] = jnp.where(lane_no == jnp.where(here, found[1:2], -1.0), 1.0, 0.0).astype(BF16)

    mk("own")

    def own_slots():
        for i in range(G):
            mine = (ids_all[mv if i == 0 else partner][0:1]) - line * width
            marks = jnp.where((mine >= 0) & (mine < width), 1.0, 0.0)
            before = dot(marks.astype(BF16), tri[...])
            position = jnp.sum(marks * before, axis=0, keepdims=True)
            place_v[i] = jnp.where(turn == position, 1.0, 0.0).astype(BF16)
            marks_v[i] = marks

    def send_gradient(p):
        wide = jnp.concatenate([part[:, t * LANES:(t + 1) * LANES] for t in range(tiles)], axis=0).astype(BF16)
        half = O * G * pad // 2
        for n in range(2):
            at = slice(n * half, (n + 1) * half)
            found = dot(wide, low[:, at])
            which = high_t[:, at]
            out = jnp.zeros((ph, half), F32)
            for t in range(tiles):
                out = jnp.where(which == float(t), found[t * ph:(t + 1) * ph], out)
            out = out.astype(BF16)
            each = G * pad
            for k in range(half // each):
                send_a[p, n * (half // each) + k] = out[:, k * each:(k + 1) * each]
        targets = []
        for k, (v, q) in enumerate(owners):
            for s in samps + [ms]:
                targets.append((v, q, s, k == O - 1 and s is ms))
        for v, q, s, last in targets:
            if not last:
                send(send_a.at[p, q], recv_a.at[p, me], A + p, v, s)
        v, q, s, _ = targets[-1]

        def away():
            send(send_a.at[p, q], recv_a.at[p, me], A + p, v, s)

        other_only(away)

        def stay():
            recv_a[p, me] = send_a[p, q]

        owner_only(stay)

    def wait_sums(p):
        owner_only(lambda: got(recv_s.at[p, pl.ds(0, S * O - 1)], SM + p))
        other_only(lambda: got(recv_s.at[p, pl.ds(0, S * O)], SM + p))

    lane = lax.broadcasted_iota(jnp.int32, (ph, LANES), 1)
    sub = lax.broadcasted_iota(jnp.int32, (ph, LANES), 0)

    def length(p):
        wait_sums(p)
        total = recv_s[p, 0]
        for k in range(1, S * O):
            total = total + recv_s[p, k]
        total = jnp.broadcast_to(total, (ph, LANES))
        cross = jnp.sum(jnp.where(lane == sub, total, 0.0), axis=1, keepdims=True)
        square = jnp.sum(jnp.where(lane == sub + ph, total, 0.0), axis=1, keepdims=True)
        return cross / (square + EPSILON)

    def advance(factor, p, dst):
        for q in range(O):
            at = slice(q * chunk, (q + 1) * chunk)
            dst[:, at] = cur[:, at] - factor * recv_u[p, q].astype(F32)

    def serve(p, factor):
        got(recv_a.at[p, pl.ds(0, N - 1)], A + p)
        mk("slots")
        if p == 0:
            coef[...] = jnp.zeros(coef.shape, F32)
            coef[0, :, 0:kept] = beta_v[...]
            if G > 1:
                got(beta_two, BETA)
                coef[1, :, 0:kept] = beta_two[...]
                got(inv.at[1], INV)
        for i in range(G):
            at = slice(i * pad, (i + 1) * pad)
            stack = []
            for v in range(V):
                val = recv_a[p, v, :, at].astype(F32)
                for s in range(1, S):
                    val = val + recv_a[p, s * V + v, :, at].astype(F32)
                high = val.astype(BF16).astype(F32)
                stack += [high, val - high]
            found = dot(jnp.concatenate(stack, axis=0).astype(BF16), place_v[i])
            slots = jnp.zeros((ph, fit), F32)
            for v in range(V):
                both = found[2 * v * ph:(2 * v + 1) * ph] + found[(2 * v + 1) * ph:(2 * v + 2) * ph]
                slots = slots + marks_v[i, v:v + 1] * both
            slots = slots * inv_root
            if p > 0:
                slots = grad[i] - factor * slots
                coef[i] = coef[i] + factor * direct[p - 1, i].astype(F32)
            grad[i] = slots
            inner = slots - PENALTY * coef[i]
            for b in range(blocks):
                cut = slice(b * bsize, (b + 1) * bsize)
                direct[p, i, :, cut] = joined(dot(split(inner[:, cut]), inv[i, b], NT)).astype(BF16)
            way = direct[p, i].astype(F32)
            spread = jnp.concatenate([way * marks_v[i, v:v + 1] for v in range(V)], axis=0).astype(BF16)
            back = dot(spread, place_v[i], NT).astype(BF16)
            for v in range(V):
                send_b[p, v, :, at] = back[v * ph:(v + 1) * ph]
        for v in all_var:
            send(send_b.at[p, v], recv_b.at[p, my_q], B + p, v, ms)
        if G > 1:
            send(direct.at[p, 1], recv_d.at[p], D + p, partner, ms)
        recv_b[p, my_q] = send_b[p, mv]

    def reduce(p):
        got(recv_c.at[p, pl.ds(0, V - 1)], C + p)
        mk("sumC")
        val = recv_c[p, 0].astype(F32)
        for v in range(1, V):
            val = val + recv_c[p, v].astype(F32)
        low_u = (val * inv_root).astype(BF16)
        recv_u[p, my_q] = low_u
        for v in all_var:
            send(recv_u.at[p, my_q], recv_u.at[p, my_q], U + p, v, ms, UQ + p * O + my_q)
        upd = low_u.astype(F32)
        now = cur[:, pl.ds(pl.multiple_of(my_q * chunk, chunk), chunk)]
        cross = jnp.sum(now * upd, axis=1, keepdims=True)
        square = jnp.sum(upd * upd, axis=1, keepdims=True)
        both = jnp.where(lane == sub, cross, jnp.where(lane == sub + ph, square, 0.0))
        slot = ms * O + my_q
        recv_s[p, slot] = jnp.sum(both, axis=0, keepdims=True)
        for v in all_var:
            for s in samps + [ms]:
                send(recv_s.at[p, slot], recv_s.at[p, slot], SM + p, v, s)
        for s in samps:
            send(recv_s.at[p, slot], recv_s.at[p, slot], SM + p, mv, s)

    owner_only(own_slots)
    factors = []
    for p in range(PASSES):
        mk("gather")
        send_gradient(p)
        mk("mid")
        if p == 0:
            for s in samps:
                send(recv_p.at[ms], recv_p.at[ms], SC, mv, s)
        if p == 1:
            got(recv_p.at[pl.ds(0, S - 1)], SC)
            val = recv_p[0]
            for s in range(1, S):
                val = val + recv_p[s]
            scores_out[...] = val * inv_root
        if p > 0:
            factors.append(length(p - 1))
        factor = factors[-1] if p else None
        mk("waitA")
        owner_only(functools.partial(serve, p, factor))
        mk("adv")
        if p > 0:
            advance(factor, p - 1, cur)
        mk("waitB")
        owner_only(lambda: got(recv_b.at[p, pl.ds(0, O - 1)], B + p))
        other_only(lambda: got(recv_b.at[p, pl.ds(0, O)], B + p))
        mk("spread")
        way = jnp.concatenate([recv_b[p, q] for q in range(O)], axis=1).astype(F32)
        which = high_t[...]
        wide = jnp.concatenate([jnp.where(which == float(t), way, 0.0) for t in range(tiles)], axis=0)
        found = dot(wide.astype(BF16), low[...], NT).astype(BF16)
        for t in range(tiles):
            d_held[:, t * LANES:(t + 1) * LANES] = found[t * ph:(t + 1) * ph]
        mk("upd")

        def piece(q):
            at = pl.ds(pl.multiple_of(q * chunk, chunk), chunk)
            return dot(x_ref[at, :], d_held[...], NT).T.astype(BF16)

        for k, (v, q) in enumerate(owners):
            if k < O - 1:
                send_c[p, k] = piece(q)
                send(send_c.at[p, k], recv_c.at[p, mv], C + p, v, ms)
            else:
                send_c[p, k] = piece(q)

                def away(k=k, v=v):
                    send(send_c.at[p, k], recv_c.at[p, mv], C + p, v, ms)

                other_only(away)

                def stay(k=k):
                    recv_c[p, mv] = send_c[p, k]

                owner_only(stay)
        mk("waitC")
        owner_only(functools.partial(reduce, p))
        mk("waitU")
        for k, (v, q) in enumerate(reversed(owners)):
            def arrive(q=q):
                got(recv_u.at[p, q], UQ + p * O + q)

            if k == 0:
                other_only(arrive)
            else:
                arrive()
            if p + 1 < PASSES:
                at = pl.ds(pl.multiple_of(q * chunk, chunk), chunk)
                new = dot(recv_u[p, q], x_ref[at, :])
                if k == 0:
                    part[...] = new
                else:
                    part[...] += new

    mk("fin")
    factors.append(length(PASSES - 1))
    factor = factors[-1]
    advance(factor, PASSES - 1, resid_out)

    def own_coef():
        coef_out[...] = coef[0] + factor * direct[PASSES - 1, 0].astype(F32)

    owner_only(own_coef)

    def edge_coef():
        val = jnp.zeros((ph, fit), F32)
        coef[0] = val
        coef[0, :, 0:kept] = beta_v[...]
        val = coef[0]
        for p in range(PASSES):
            got(recv_d.at[p], D + p)
            val = val + factors[p] * recv_d[p].astype(F32)
        coef_out[...] = val

    other_only(edge_coef)
    mk("drain")

    sent(ids_all.at[pl.ds(0, V - 1)], IDS)
    sent(recv_p.at[pl.ds(0, S - 1)], SC)

    def drain_owner():
        for p in range(PASSES):
            sent(recv_a.at[p, pl.ds(0, S * O - 1)], A + p)
            sent(send_b.at[p, pl.ds(0, V - 1)], B + p)
            if O > 1:
                sent(send_c.at[p, pl.ds(0, O - 1)], C + p)
            sent(recv_c.at[p, pl.ds(0, V - 1)], U + p)
            sent(all_rows(p), SM + p)
            if G > 1:
                sent(direct.at[p, 1], D + p)

    def all_rows(p):
        return recv_s.at[p, pl.ds(0, N - 1)]

    owner_only(drain_owner)

    def drain_other():
        sent(beta_v, BETA)
        sent(inv.at[0], INV)
        for p in range(PASSES):
            sent(recv_a.at[p, pl.ds(0, S * O)], A + p)
            sent(send_c.at[p], C + p)

    other_only(drain_other)


def on_device(geno, scale_index, scale_table, residual, beta_active, block_inverse, active_ids, admit_ids):
    V, S = lax.axis_size("var"), lax.axis_size("samp")
    N = V * S
    O, G = owners_of(V)
    rows, width = geno.shape
    ph = residual.shape[0]
    fit = active_ids.shape[0] + admit_ids.shape[0]
    pad = LANES * pl.cdiv(2 * fit // V, LANES)
    chunk = rows // O
    vmem = pl.BlockSpec(memory_space=pltpu.VMEM)
    hbm = pl.BlockSpec(memory_space=pl.ANY)
    n_send = 4 + 6 * PASSES
    n_recv = n_send + PASSES * O
    per_group = rows // scale_index.shape[0]
    return pl.pallas_call(
        functools.partial(kernel, V, S, pad),
        out_shape=(
            jax.ShapeDtypeStruct((ph, width), F32),
            jax.ShapeDtypeStruct((ph, fit), F32),
            jax.ShapeDtypeStruct((ph, rows), F32),
        ),
        in_specs=[hbm] * 8,
        out_specs=(vmem, vmem, vmem),
        scratch_shapes=[
            pltpu.VMEM((rows, width), BF16),
            pltpu.VMEM(scale_index.shape, jnp.int32),
            pltpu.SMEM(scale_table.shape, F32),
            pltpu.VMEM((ph, rows), F32),
            pltpu.VMEM(beta_active.shape, F32),
            pltpu.VMEM(block_inverse.shape, F32),
            pltpu.VMEM((1, active_ids.shape[0]), jnp.int32),
            pltpu.VMEM((1, admit_ids.shape[0]), jnp.int32),
            pltpu.VMEM(scale_index.shape, F32),
            pltpu.VMEM((ph, rows), BF16),
            pltpu.VMEM((ph, width), F32),
            pltpu.VMEM((LANES, V * pad), BF16),
            pltpu.VMEM((ph, V * pad), F32),
            pltpu.VMEM((G, V, fit), F32),
            pltpu.VMEM((G, pad, fit), BF16),
            pltpu.VMEM((fit, fit), BF16),
            pltpu.VMEM((G,) + block_inverse.shape, BF16),
            pltpu.VMEM(beta_active.shape, F32),
            pltpu.VMEM((V, 1, fit), jnp.int32),
            pltpu.VMEM((ph, width), BF16),
            pltpu.VMEM((G, ph, fit), F32),
            pltpu.VMEM((G, ph, fit), F32),
            pltpu.VMEM((PASSES, G, ph, fit), BF16),
            pltpu.VMEM((PASSES, O, ph, G * pad), BF16),
            pltpu.VMEM((PASSES, N, ph, G * pad), BF16),
            pltpu.VMEM((PASSES, V, ph, G * pad), BF16),
            pltpu.VMEM((PASSES, O, ph, G * pad), BF16),
            pltpu.VMEM((PASSES, O, ph, chunk), BF16),
            pltpu.VMEM((PASSES, V, ph, chunk), BF16),
            pltpu.VMEM((PASSES, O, ph, chunk), BF16),
            pltpu.VMEM((S, ph, width), F32),
            pltpu.VMEM((PASSES, N, 1, LANES), F32),
            pltpu.VMEM((PASSES, ph, fit), BF16),
            pltpu.SemaphoreType.DMA((rows // (2 * per_group),)),
            pltpu.SemaphoreType.DMA((7,)),
            pltpu.SemaphoreType.DMA((n_send,)),
            pltpu.SemaphoreType.DMA((n_recv,)),
        ],
        compiler_params=pltpu.CompilerParams(
            collective_id=0, has_side_effects=True, vmem_limit_bytes=60 * 1024 * 1024
        ),
    )(geno, scale_index, scale_table, residual, beta_active, block_inverse, active_ids[None], admit_ids[None])


def solution(mesh):
    placed = (
        P("samp", "var"), P("samp", "var"), P(), P(None, "samp"), P(None, "var"),
        P("var", None, None), P("var"), P("var"),
    )
    return jax.shard_map(
        on_device, mesh=mesh, in_specs=placed,
        out_specs=(P(None, "var"), P(None, "var"), P(None, "samp")), check_vma=False,
    )
```

time: 90 us -> 82.1 us (0.912)
  Pallas kernels: 84.8 us -> 77 us
    pallas_call x1, Pallas kernels: 84.8 us -> 77 us  [on_device(): pl.pallas_call(functools.partial(kernel, V, S, pad), out_shape=(jax.Shape...]
where the time goes in v1:
time: 82.1 us; the launch traced here: 81.9 us
  Pallas kernels  77 us (94%)
  local copies, waits for them, and re-layouts  4.27 us (5%)
    pallas_call x1, Pallas kernels, on_device(): pl.pallas_call(functools.partial(kernel, V, S, pad), out_shape=(jax.Shape...  77 us
    unnamed x3, local copies, waits for them, and re-layouts  4.27 us

profile of v1, /device:TPU:0, one launch (start us, length us, event | category | flops | bytes accessed | tf_op | source)
XLA Modules:
  0.0 81.9 jit_solution(9001362525263416682)
XLA Ops:
  0.6 77.0 %shard_map.103 = (f32[8,2048]{1,0:T(8,128)}, f32[8,512]{1,0:T(8,128)}, f32[8,2048]{1,0:T(8,128)}) custom-call(bf16[2048,2048]{1,0:T(8,128)(2,1)} %geno.1, s32[16,2048]{1,0:T(8,128)} %sidx.1, f32[16]{0:T(128)} %table.1, f32[8,2048]{1,0:T(8,128)} %resid.1, f32[8,448]{1,0:T(8,128)} %beta.1, f32[2,256,256]{2,1,0:T(8,128)} %binv.1, s32[1,448]{1,0:T(1,128)} %bitcast.2, ...), custom_call_target="tpu_custom_call" | custom-call | tf_op jit(solution)/shard_map/pallas_call | solution.py:529
  77.6 1.5 %copy.14 = f32[8,2048]{1,0:T(8,128)} copy(f32[8,2048]{1,0:T(8,128)} %get-tuple-element.6) | data formatting | bytes 131072
  79.1 1.3 %copy.15 = f32[8,512]{1,0:T(8,128)} copy(f32[8,512]{1,0:T(8,128)} %get-tuple-element.7) | data formatting | bytes 32768
  80.4 1.5 %copy.16 = f32[8,2048]{1,0:T(8,128)} copy(f32[8,2048]{1,0:T(8,128)} %get-tuple-element.8) | data formatting | bytes 131072

commit v2 on v1

--- a/solution.py
+++ b/solution.py
@@ -52,7 +52,7 @@
     V, S, pad,
     geno, sidx, table, resid, beta, binv, active, admit,
     scores_out, coef_out, resid_out,
-    x_ref, sidx_v, table_s, cur, beta_v, binv_v, act_v, adm_v,
+    x_ref, xt_ref, sidx_v, table_s, cur, beta_v, binv_v, act_v, adm_v,
     scale_ref, rlow, part, low, high_t, marks_v, place_v, tri, inv, beta_two, ids_all,
     d_held, coef, grad, direct,
     send_a, recv_a, send_b, recv_b, send_c, recv_c, recv_u, recv_p, recv_s, recv_d,
@@ -75,8 +75,12 @@
     fit = kept + adm_v.shape[1]
     blocks, bsize = binv_v.shape[0], binv_v.shape[1]
     chunk = rows // O
+    join = G
     tiles = width // LANES
-    step = 2 * per_group
+    piece = 2 * per_group
+    n_loads = rows // piece
+    per_step = 2 if n_loads % 2 == 0 else 1
+    step = per_step * piece
     n_steps = rows // step
     inv_root = 1.0 / math.sqrt(rows * S)
     mv, ms = lax.axis_index("var"), lax.axis_index("samp")
@@ -85,19 +89,19 @@
     mk("greet")
     barrier = pltpu.get_barrier_semaphore()
 
-    def greet(k, c):
-        t = lax.rem(me + k, N)
-        pl.semaphore_signal(
-            barrier, inc=1, device_id={"var": lax.rem(t, V), "samp": lax.div(t, V)},
-            device_id_type=pl.DeviceIdType.MESH,
-        )
-        return c
-
-    lax.fori_loop(1, N, greet, 0)
+    samps = [lax.rem(ms + d, S) for d in range(1, S)] + [ms]
+    if S == 4:
+        samps = [3 - ms] + [ms + d - 2 * d * lax.rem(lax.div(ms, d), 2) for d in (2, 1)] + [ms]
+    others = [lax.rem(mv + d, V) for d in range(V - 1, -1, -1)]
+    for s in samps:
+        for v in others[:-1] if s is ms else others:
+            pl.semaphore_signal(
+                barrier, inc=1, device_id={"var": v, "samp": s}, device_id_type=pl.DeviceIdType.MESH
+            )
     mk("start")
 
     def load(i):
-        at = pl.ds(pl.multiple_of(i * step, step), step)
+        at = pl.ds(pl.multiple_of(i * piece, piece), piece)
         return pltpu.make_async_copy(geno.at[at], x_ref.at[at], load_sem.at[i])
 
     small = [(table, table_s), (sidx, sidx_v), (resid, cur), (active, act_v), (admit, adm_v), (beta, beta_v), (binv, binv_v)]
@@ -105,11 +109,6 @@
     for c in pulls[:5]:
         c.start()
     load(0).start()
-    load(1).start()
-    for c in pulls[5:]:
-        c.start()
-    for i in range(2, n_steps):
-        load(i).start()
 
     if G == 1:
         is_owner, my_q = None, mv
@@ -132,7 +131,7 @@
         zs = [side * 3 + (1 - 2 * side) * k for k in (3, 2, 1 - z0, z0)]
         all_var = [8 * hh + 2 * zz + cc for hh in hs for zz in zs for cc in cores][:-1]
         partner = 8 * h + 2 * (side * 3 + (1 - 2 * side) * (1 - z0)) + c0
-    samps = [lax.rem(ms + d, S) for d in range(1, S)]
+    samps = samps[:-1]
 
     def owner_only(fn):
         if G == 1:
@@ -166,9 +165,15 @@
     U = D + PASSES
     UQ = U + PASSES
 
-    mk("setup")
+    mk("inputs")
     for c in pulls[:5]:
         c.wait()
+    mk("setup")
+    for i in range(1, n_loads):
+        if i == n_loads // 2:
+            for c in pulls[5:]:
+                c.start()
+        load(i).start()
     ids_all[mv, :, 0:kept] = act_v[...]
     ids_all[mv, :, kept:fit] = adm_v[...]
     index = sidx_v[...]
@@ -181,21 +186,23 @@
     cols = 256
 
     def screen(i, c):
-        load(i).wait()
+        for k in range(per_step):
+            load(i * per_step + k).wait()
         at = pl.ds(pl.multiple_of(i * step, step), step)
         left = rlow[:, at]
         for j in range(width // cols):
             lane = slice(j * cols, (j + 1) * cols)
             block = []
-            for half in range(2):
-                sub = pl.ds(pl.multiple_of(i * step + half * per_group, per_group), per_group)
-                block.append(x_ref[sub, lane].astype(F32) * scale_ref[pl.ds(2 * i + half, 1), lane])
+            for n in range(step // per_group):
+                sub = pl.ds(pl.multiple_of(i * step + n * per_group, per_group), per_group)
+                scale = scale_ref[pl.ds(i * (step // per_group) + n, 1), lane]
+                block.append(x_ref[sub, lane].astype(F32) * scale)
             block = jnp.concatenate(block, axis=0).astype(BF16)
             x_ref[at, lane] = block
             part[:, lane] += dot(left, block)
         return c
 
-    first = (n_steps * 5) // 8
+    first = (n_steps * 3) // 4
     mk("screen1")
     lax.fori_loop(0, first, screen, 0)
     mk("inv")
@@ -253,9 +260,10 @@
         high_t[:, at] = jnp.broadcast_to(jnp.where(here, found[0:1], -1.0), (ph, pad))
         low[:, at] = jnp.where(lane_no == jnp.where(here, found[1:2], -1.0), 1.0, 0.0).astype(BF16)
 
-    mk("own")
+    mk(None)
 
     def own_slots():
+        mk("own")
         for i in range(G):
             mine = (ids_all[mv if i == 0 else partner][0:1]) - line * width
             marks = jnp.where((mine >= 0) & (mine < width), 1.0, 0.0)
@@ -263,6 +271,7 @@
             position = jnp.sum(marks * before, axis=0, keepdims=True)
             place_v[i] = jnp.where(turn == position, 1.0, 0.0).astype(BF16)
             marks_v[i] = marks
+        mk(None)
 
     def send_gradient(p):
         wide = jnp.concatenate([part[:, t * LANES:(t + 1) * LANES] for t in range(tiles)], axis=0).astype(BF16)
@@ -320,8 +329,9 @@
             dst[:, at] = cur[:, at] - factor * recv_u[p, q].astype(F32)
 
     def serve(p, factor):
+        mk("gotA")
         got(recv_a.at[p, pl.ds(0, N - 1)], A + p)
-        mk("slots")
+        mk("serve")
         if p == 0:
             coef[...] = jnp.zeros(coef.shape, F32)
             coef[0, :, 0:kept] = beta_v[...]
@@ -357,13 +367,16 @@
             back = dot(spread, place_v[i], NT).astype(BF16)
             for v in range(V):
                 send_b[p, v, :, at] = back[v * ph:(v + 1) * ph]
+        mk("sendB")
         for v in all_var:
             send(send_b.at[p, v], recv_b.at[p, my_q], B + p, v, ms)
         if G > 1:
             send(direct.at[p, 1], recv_d.at[p], D + p, partner, ms)
         recv_b[p, my_q] = send_b[p, mv]
+        mk(None)
 
     def reduce(p):
+        mk("gotC")
         got(recv_c.at[p, pl.ds(0, V - 1)], C + p)
         mk("sumC")
         val = recv_c[p, 0].astype(F32)
@@ -373,6 +386,7 @@
         recv_u[p, my_q] = low_u
         for v in all_var:
             send(recv_u.at[p, my_q], recv_u.at[p, my_q], U + p, v, ms, UQ + p * O + my_q)
+        mk("sums")
         upd = low_u.astype(F32)
         now = cur[:, pl.ds(pl.multiple_of(my_q * chunk, chunk), chunk)]
         cross = jnp.sum(now * upd, axis=1, keepdims=True)
@@ -385,6 +399,16 @@
                 send(recv_s.at[p, slot], recv_s.at[p, slot], SM + p, v, s)
         for s in samps:
             send(recv_s.at[p, slot], recv_s.at[p, slot], SM + p, mv, s)
+        mk(None)
+
+    turned = 2 * LANES
+
+    def turn_rows(i, c):
+        at = pl.ds(pl.multiple_of(i * turned, turned), turned)
+        for j in range(width // turned):
+            cut = slice(j * turned, (j + 1) * turned)
+            xt_ref[cut, at] = x_ref[at, cut].T
+        return c
 
     owner_only(own_slots)
     factors = []
@@ -395,6 +419,9 @@
         if p == 0:
             for s in samps:
                 send(recv_p.at[ms], recv_p.at[ms], SC, mv, s)
+            mk("turn")
+            lax.fori_loop(0, rows // turned, turn_rows, 0)
+            mk("mid")
         if p == 1:
             got(recv_p.at[pl.ds(0, S - 1)], SC)
             val = recv_p[0]
@@ -404,7 +431,7 @@
         if p > 0:
             factors.append(length(p - 1))
         factor = factors[-1] if p else None
-        mk("waitA")
+        mk(None)
         owner_only(functools.partial(serve, p, factor))
         mk("adv")
         if p > 0:
@@ -421,27 +448,27 @@
             d_held[:, t * LANES:(t + 1) * LANES] = found[t * ph:(t + 1) * ph]
         mk("upd")
 
-        def piece(q):
-            at = pl.ds(pl.multiple_of(q * chunk, chunk), chunk)
-            return dot(x_ref[at, :], d_held[...], NT).T.astype(BF16)
-
         for k, (v, q) in enumerate(owners):
+            if k % join == 0:
+                at = pl.ds(pl.multiple_of(lax.div(q, join) * (join * chunk), join * chunk), join * chunk)
+                wide = dot(d_held[...], xt_ref[:, at]).astype(BF16)
+                first_q = lax.div(q, join) * join
+                for i in range(join):
+                    send_c[p, first_q + i] = wide[:, i * chunk:(i + 1) * chunk]
             if k < O - 1:
-                send_c[p, k] = piece(q)
-                send(send_c.at[p, k], recv_c.at[p, mv], C + p, v, ms)
+                send(send_c.at[p, q], recv_c.at[p, mv], C + p, v, ms)
             else:
-                send_c[p, k] = piece(q)
-
-                def away(k=k, v=v):
-                    send(send_c.at[p, k], recv_c.at[p, mv], C + p, v, ms)
+
+                def away(q=q, v=v):
+                    send(send_c.at[p, q], recv_c.at[p, mv], C + p, v, ms)
 
                 other_only(away)
 
-                def stay(k=k):
-                    recv_c[p, mv] = send_c[p, k]
+                def stay(q=q):
+                    recv_c[p, mv] = send_c[p, q]
 
                 owner_only(stay)
-        mk("waitC")
+        mk(None)
         owner_only(functools.partial(reduce, p))
         mk("waitU")
         for k, (v, q) in enumerate(reversed(owners)):
@@ -452,10 +479,11 @@
                 other_only(arrive)
             else:
                 arrive()
-            if p + 1 < PASSES:
-                at = pl.ds(pl.multiple_of(q * chunk, chunk), chunk)
-                new = dot(recv_u[p, q], x_ref[at, :])
-                if k == 0:
+            if p + 1 < PASSES and k % join == join - 1:
+                first_q = lax.div(q, join) * join
+                at = pl.ds(pl.multiple_of(first_q * chunk, join * chunk), join * chunk)
+                new = dot(jnp.concatenate([recv_u[p, first_q + i] for i in range(join)], axis=1), x_ref[at, :])
+                if k == join - 1:
                     part[...] = new
                 else:
                     part[...] += new
@@ -526,17 +554,14 @@
     n_send = 4 + 6 * PASSES
     n_recv = n_send + PASSES * O
     per_group = rows // scale_index.shape[0]
-    return pl.pallas_call(
+    out = pl.pallas_call(
         functools.partial(kernel, V, S, pad),
-        out_shape=(
-            jax.ShapeDtypeStruct((ph, width), F32),
-            jax.ShapeDtypeStruct((ph, fit), F32),
-            jax.ShapeDtypeStruct((ph, rows), F32),
-        ),
+        out_shape=(pltpu.VMEM((ph, width), F32), pltpu.VMEM((ph, fit), F32), pltpu.VMEM((ph, rows), F32)),
         in_specs=[hbm] * 8,
         out_specs=(vmem, vmem, vmem),
         scratch_shapes=[
             pltpu.VMEM((rows, width), BF16),
+            pltpu.VMEM((width, rows), BF16),
             pltpu.VMEM(scale_index.shape, jnp.int32),
             pltpu.SMEM(scale_table.shape, F32),
             pltpu.VMEM((ph, rows), F32),
@@ -579,6 +604,17 @@
         ),
     )(geno, scale_index, scale_table, residual, beta_active, block_inverse, active_ids[None], admit_ids[None])
 
+    def hand_out(*refs):
+        half = len(refs) // 2
+        for a, b in zip(refs[:half], refs[half:]):
+            b[...] = a[...]
+
+    return pl.pallas_call(
+        hand_out, out_shape=tuple(jax.ShapeDtypeStruct(o.shape, o.dtype) for o in out),
+        in_specs=[vmem] * 3, out_specs=(vmem,) * 3,
+        compiler_params=pltpu.CompilerParams(vmem_limit_bytes=1024 * 1024),
+    )(*out)
+
 
 def solution(mesh):
     placed = (

time: 82.1 us -> 66.1 us (0.81)
  Pallas kernels: 77 us -> 65.3 us
  local copies, waits for them, and re-layouts: 4.27 us -> 0 us
    pallas_call x1 -> x2, Pallas kernels: 77 us -> 65.3 us  [the longest x1 64.6 us: on_device(): pl.pallas_call(functools.partial(kernel, V, S, pad), out_shape=(pltpu.VME...]
    unnamed x3 -> x0, local copies, waits for them, and re-layouts: 4.27 us -> none
where the time goes in v2:
time: 66.1 us; the launch traced here: 66 us
  Pallas kernels  65.3 us (99%)
    pallas_call x1, Pallas kernels, on_device(): pl.pallas_call(functools.partial(kernel, V, S, pad), out_shape=(pltpu.VME...  64.6 us

profile of v2, /device:TPU:0, one launch (start us, length us, event | category | flops | bytes accessed | tf_op | source)
XLA Modules:
  0.0 66.0 jit_solution(9094191823674448197)
XLA Ops:
  0.6 64.6 %shard_map.103 = (f32[8,2048]{1,0:T(8,128)S(1)}, f32[8,512]{1,0:T(8,128)S(1)}, f32[8,2048]{1,0:T(8,128)S(1)}) custom-call(bf16[2048,2048]{1,0:T(8,128)(2,1)} %geno.1, s32[16,2048]{1,0:T(8,128)} %sidx.1, f32[16]{0:T(128)} %table.1, f32[8,2048]{1,0:T(8,128)} %resid.1, f32[8,448]{1,0:T(8,128)} %beta.1, f32[2,256,256]{2,1,0:T(8,128)} %binv.1, s32[1,448]{1,0:T(1,128)} %bitcast.2, ...), custom_call_target="tpu_custom_call" | custom-call | tf_op jit(solution)/shard_map/pallas_call | solution.py:557
  65.3 0.7 %shard_map.104 = (f32[8,2048]{1,0:T(8,128)}, f32[8,512]{1,0:T(8,128)}, f32[8,2048]{1,0:T(8,128)}) custom-call(f32[8,2048]{1,0:T(8,128)S(1)} %get-tuple-element.6.refs_0_, f32[8,512]{1,0:T(8,128)S(1)} %get-tuple-element.7.refs_1_, f32[8,2048]{1,0:T(8,128)S(1)} %get-tuple-element.8.refs_2_), custom_call_target="tpu_custom_call" | custom-call | tf_op jit(solution)/shard_map/pallas_call | solution.py:612

commit v3 on v2

v3 whole, which is shorter than its diff:
```python
import functools
import math

import jax
import jax.numpy as jnp
from jax import lax
from jax.experimental import pallas as pl
from jax.experimental.pallas import tpu as pltpu
from jax.sharding import PartitionSpec as P

PASSES = 3
PENALTY = 0.5
EPSILON = 1e-06
LANES = 128
F32 = jnp.float32
BF16 = jnp.bfloat16
NN = (((1,), (0,)), ((), ()))
NT = (((1,), (1,)), ((), ()))


def dot(a, b, dims=NN):
    return lax.dot_general(a, b, dims, preferred_element_type=F32)


def split(x):
    high = x.astype(BF16).astype(F32)
    return jnp.concatenate([high, x - high], axis=0).astype(BF16)


def joined(x):
    half = x.shape[0] // 2
    return x[:half] + x[half:]


def kernel(
    V, S, pad,
    geno, sidx, table, resid, beta, binv, active, admit,
    scores_out, coef_out, resid_out,
    x_ref, xt_ref, sidx_v, table_s, cur, beta_v, binv_v, act_v, adm_v,
    scale_ref, rlow, part, low, high_t, marks_v, place_v, tri, inv, beta_two, ids_all, blank,
    d_held, coef, grad, direct,
    send_a, recv_a, send_b, recv_b, send_c, recv_c, recv_u, recv_p, recv_s, recv_d,
    load_sem, in_sem, send_sem, recv_sem,
):
    cur_scope = [None]

    def mk(name):
        pass

    N = V * S
    H, O = V // 8, V // 4
    rows, width = x_ref.shape
    groups = sidx_v.shape[0]
    per_group = rows // groups
    levels = table_s.shape[0]
    ph = cur.shape[0]
    kept = act_v.shape[1]
    fit = kept + adm_v.shape[1]
    blocks, bsize = binv_v.shape[0], binv_v.shape[1]
    chunk = rows // O
    tiles = width // LANES
    piece = 2 * per_group
    n_loads = rows // piece
    per_step = 2 if n_loads % 2 == 0 else 1
    step = per_step * piece
    n_steps = rows // step
    inv_root = 1.0 / math.sqrt(rows * S)
    mv, ms = lax.axis_index("var"), lax.axis_index("samp")
    me = ms * V + mv

    mk("greet")
    barrier = pltpu.get_barrier_semaphore()

    samps = [lax.rem(ms + d, S) for d in range(1, S)] + [ms]
    if S == 4:
        samps = [3 - ms] + [ms + d - 2 * d * lax.rem(lax.div(ms, d), 2) for d in (2, 1)] + [ms]
    others = [lax.rem(mv + d, V) for d in range(V - 1, -1, -1)]
    for s in samps:
        for v in others[:-1] if s is ms else others:
            pl.semaphore_signal(
                barrier, inc=1, device_id={"var": v, "samp": s}, device_id_type=pl.DeviceIdType.MESH
            )
    mk("start")

    def load(i):
        at = pl.ds(pl.multiple_of(i * piece, piece), piece)
        return pltpu.make_async_copy(geno.at[at], x_ref.at[at], load_sem.at[i])

    small = [(table, table_s), (sidx, sidx_v), (resid, cur), (active, act_v), (admit, adm_v), (beta, beta_v), (binv, binv_v)]
    pulls = [pltpu.make_async_copy(a, b, in_sem.at[i]) for i, (a, b) in enumerate(small)]
    for c in pulls[:5]:
        c.start()
    load(0).start()
    load(1).start()

    h, z, c0 = lax.div(mv, 8), lax.rem(lax.div(mv, 2), 4), lax.rem(mv, 2)
    side = lax.div(z, 2)
    hs = [lax.rem(h + d, H) for d in range(1, H)] + [h]
    halves = [(hh, ss) for hh in hs for ss in (1 - side, side)]
    owners = [(8 * hh + 2 * (1 + ss) + 1, 2 * hh + ss) for hh, ss in halves]
    is_owner = jnp.logical_and(z == 1 + side, c0 == 1)
    my_q = 2 * h + side
    my_g = 8 * h + 4 * side + lax.rem(ms, 4)
    serves = jnp.logical_and(is_owner, ms < 4)
    own_turn = ms == 2 * lax.rem(z, 2) + c0
    keeps = jnp.logical_and(is_owner, own_turn)
    gives = jnp.logical_and(own_turn, jnp.logical_not(is_owner))
    taker = 8 * h + 2 * (1 + side) + 1
    z0 = z + side * (3 - 2 * z)
    zs = [side * 3 + (1 - 2 * side) * k for k in (3, 2, 1 - z0, z0)]
    all_var = [8 * hh + 2 * zz + cc for hh in hs for zz in zs for cc in (1 - c0, c0)][:-1]
    samps = samps[:-1]

    def owner_only(fn):
        pl.when(is_owner)(fn)

    def other_only(fn):
        pl.when(jnp.logical_not(is_owner))(fn)

    def unless(cond, fn):
        pl.when(jnp.logical_not(cond))(fn)

    def send(src, dst, sem, v, s, r_sem=None):
        pltpu.make_async_remote_copy(
            src_ref=src, dst_ref=dst, send_sem=send_sem.at[sem],
            recv_sem=recv_sem.at[sem if r_sem is None else r_sem],
            device_id={"var": v, "samp": s}, device_id_type=pl.DeviceIdType.MESH,
        ).start()

    def got(ref, sem):
        pltpu.make_async_copy(ref, ref, recv_sem.at[sem]).wait()

    def sent(ref, sem):
        pltpu.make_async_copy(ref, ref, send_sem.at[sem]).wait()

    IDS, INV, BETA, SC = 0, 1, 2, 3
    A = 4
    B = A + PASSES
    C = B + PASSES
    SM = C + PASSES
    D = SM + PASSES
    U = D + PASSES
    UQ = U + PASSES

    tri[...] = jnp.where(
        lax.broadcasted_iota(jnp.int32, (fit, fit), 0) < lax.broadcasted_iota(jnp.int32, (fit, fit), 1),
        1.0, 0.0,
    ).astype(BF16)
    part[...] = jnp.zeros((ph, width), F32)
    mk("inputs")
    for c in pulls[:5]:
        c.wait()
    mk("setup")
    for i in range(2, n_loads):
        if i == n_loads // 2:
            for c in pulls[5:]:
                c.start()
        load(i).start()
    ids_all[mv, :, 0:kept] = act_v[...]
    ids_all[mv, :, kept:fit] = adm_v[...]
    index = sidx_v[...]
    scales = jnp.zeros(index.shape, F32)
    for level in range(levels):
        scales = jnp.where(index == level, table_s[level], scales)
    scale_ref[...] = scales
    rlow[...] = cur[...].astype(BF16)
    cols = 256

    def screen(i, c):
        for k in range(per_step):
            load(i * per_step + k).wait()
        at = pl.ds(pl.multiple_of(i * step, step), step)
        left = rlow[:, at]
        for j in range(width // cols):
            lane = slice(j * cols, (j + 1) * cols)
            block = []
            for n in range(step // per_group):
                sub = pl.ds(pl.multiple_of(i * step + n * per_group, per_group), per_group)
                scale = scale_ref[pl.ds(i * (step // per_group) + n, 1), lane]
                block.append(x_ref[sub, lane].astype(F32) * scale)
            block = jnp.concatenate(block, axis=0).astype(BF16)
            x_ref[at, lane] = block
            part[:, lane] += dot(left, block)
        return c

    first = pl.cdiv(n_steps, 4)
    mk("screen1")
    lax.fori_loop(0, first, screen, 0)
    mk("barrier")
    pl.semaphore_wait(barrier, N - 1)
    for v in all_var:
        send(ids_all.at[mv], ids_all.at[mv], IDS, v, ms)

    mk("screen2")
    lax.fori_loop(first, n_steps, screen, 0)
    recv_p[ms] = part[...]
    mk("inv")
    for c in pulls[5:]:
        c.wait()
    for b in range(blocks):
        inv[0, b] = binv_v[b].astype(BF16)

    def hand_over():
        send(beta_v, beta_two, BETA, taker, ms)
        send(inv.at[0], inv.at[1], INV, taker, ms)

    pl.when(gives)(hand_over)

    def keep():
        beta_two[...] = beta_v[...]
        inv[1] = inv[0]

    pl.when(keeps)(keep)
    mk("idswait")
    got(ids_all.at[pl.ds(0, V - 1)], IDS)
    mk("idsproc")
    line = lax.broadcasted_iota(jnp.int32, (V, fit), 0)

    def lines(g):
        return ids_all[g, 0:1, :]

    all_ids = jnp.zeros((V, fit), jnp.int32)
    for g in range(V):
        all_ids = jnp.where(line == g, lines(g), all_ids)
    column = all_ids - mv * width
    held = (column >= 0) & (column < width)
    serial = dot(jnp.where(held, 1.0, 0.0).astype(BF16), tri[...])
    serial = jnp.where(held, serial, -1.0)
    column = jnp.where(held, column, 0)
    eight = lax.broadcasted_iota(jnp.int32, (8, fit), 0)
    turn = lax.broadcasted_iota(jnp.int32, (pad, fit), 0).astype(F32)
    lane_no = lax.broadcasted_iota(jnp.int32, (LANES, pad), 0).astype(F32)
    for g in range(V):
        col = column[g:g + 1]
        digits = jnp.where(
            eight == 0, lax.shift_right_logical(col, 7),
            jnp.where(eight == 1, col & 127, jnp.where(eight == 2, 1, 0)),
        ).astype(F32).astype(BF16)
        place = jnp.where(turn == serial[g:g + 1], 1.0, 0.0).astype(BF16)
        found = dot(digits, place, NT)
        here = found[2:3] > 0.5
        at = slice(g * pad, (g + 1) * pad)
        high_t[:, at] = jnp.broadcast_to(jnp.where(here, found[0:1], -1.0), (ph, pad))
        low[:, at] = jnp.where(lane_no == jnp.where(here, found[1:2], -1.0), 1.0, 0.0).astype(BF16)

    mk(None)

    def own_slots():
        mk("own")
        mine = ids_all[my_g][0:1] - line * width
        marks = jnp.where((mine >= 0) & (mine < width), 1.0, 0.0)
        before = dot(marks.astype(BF16), tri[...])
        position = jnp.sum(marks * before, axis=0, keepdims=True)
        place_v[...] = jnp.where(turn == position, 1.0, 0.0).astype(BF16)
        marks_v[...] = marks
        mk(None)

    def send_gradient(p):
        wide = jnp.concatenate([part[:, t * LANES:(t + 1) * LANES] for t in range(tiles)], axis=0).astype(BF16)
        for n, (hh, ss) in enumerate(halves):
            base = 8 * hh + 4 * ss
            at = pl.ds(pl.multiple_of(base * pad, 4 * pad), 4 * pad)
            found = dot(wide, low[:, at])
            which = high_t[:, at]
            out = jnp.zeros((ph, 4 * pad), F32)
            for t in range(tiles):
                out = jnp.where(which == float(t), found[t * ph:(t + 1) * ph], out)
            out = out.astype(BF16)
            for k in range(4):
                send_a[p, base + k] = out[:, k * pad:(k + 1) * pad]
            v = 8 * hh + 2 * (1 + ss) + 1
            last = n == len(halves) - 1
            turns = [lax.rem(ms + d, 4) for d in (2, 3, 1)]
            for r in turns if last else turns + [lax.rem(ms, 4)]:
                send(send_a.at[p, base + r], recv_a.at[p, me], A + p, v, r)

        def away():
            send(send_a.at[p, my_g], recv_a.at[p, me], A + p, taker, lax.rem(ms, 4))

        unless(serves, away)

        def stay():
            recv_a[p, me] = send_a[p, my_g]

        pl.when(serves)(stay)

    def wait_sums(p):
        owner_only(lambda: got(recv_s.at[p, pl.ds(0, S * O - 1)], SM + p))
        other_only(lambda: got(recv_s.at[p, pl.ds(0, S * O)], SM + p))

    lane = lax.broadcasted_iota(jnp.int32, (ph, LANES), 1)
    sub = lax.broadcasted_iota(jnp.int32, (ph, LANES), 0)

    def length(p):
        wait_sums(p)
        total = recv_s[p, 0]
        for k in range(1, S * O):
            total = total + recv_s[p, k]
        total = jnp.broadcast_to(total, (ph, LANES))
        cross = jnp.sum(jnp.where(lane == sub, total, 0.0), axis=1, keepdims=True)
        square = jnp.sum(jnp.where(lane == sub + ph, total, 0.0), axis=1, keepdims=True)
        return cross / (square + EPSILON)

    def advance(factor, p, dst):
        for q in range(O):
            at = slice(q * chunk, (q + 1) * chunk)
            dst[:, at] = cur[:, at] - factor * recv_u[p, q].astype(F32)

    def serve(p, factor):
        mk("gotA")
        got(recv_a.at[p, pl.ds(0, N - 1)], A + p)
        mk("serve")
        if p == 0:
            def take():
                got(beta_two, BETA)
                got(inv.at[1], INV)

            unless(keeps, take)
            coef[...] = jnp.zeros(coef.shape, F32)
            coef[:, 0:kept] = beta_two[...]
        stack = []
        for v in range(V):
            val = recv_a[p, v].astype(F32)
            for s in range(1, S):
                val = val + recv_a[p, s * V + v].astype(F32)
            high = val.astype(BF16).astype(F32)
            stack += [high, val - high]
        found = dot(jnp.concatenate(stack, axis=0).astype(BF16), place_v[...])
        slots = jnp.zeros((ph, fit), F32)
        for v in range(V):
            both = found[2 * v * ph:(2 * v + 1) * ph] + found[(2 * v + 1) * ph:(2 * v + 2) * ph]
            slots = slots + marks_v[v:v + 1] * both
        slots = slots * inv_root
        if p > 0:
            slots = grad[...] - factor * slots
            coef[...] = coef[...] + factor * direct[p - 1].astype(F32)
        grad[...] = slots
        inner = slots - PENALTY * coef[...]
        ways = []
        for b in range(blocks):
            cut = slice(b * bsize, (b + 1) * bsize)
            ways.append(joined(dot(split(inner[:, cut]), inv[1, b], NT)).astype(BF16))
        way = jnp.concatenate(ways, axis=1)
        direct[p] = way
        way = way.astype(F32)
        spread = jnp.concatenate([way * marks_v[v:v + 1] for v in range(V)], axis=0).astype(BF16)
        back = dot(spread, place_v[...], NT).astype(BF16)
        for v in range(V):
            send_b[p, v] = back[v * ph:(v + 1) * ph]
        mk("sendB")
        for s in samps + [ms]:
            for v in all_var:
                send(send_b.at[p, v], recv_b.at[p, my_g], B + p, v, s)
        for s in samps:
            send(send_b.at[p, mv], recv_b.at[p, my_g], B + p, mv, s)
        recv_b[p, my_g] = send_b[p, mv]
        for s in samps:
            send(direct.at[p], recv_d.at[p], D + p, my_g, s)

        def away():
            send(direct.at[p], recv_d.at[p], D + p, my_g, ms)

        unless(keeps, away)

        def stay():
            recv_d[p] = direct[p]

        pl.when(keeps)(stay)
        mk(None)

    def reduce(p):
        mk("gotC")
        got(recv_c.at[p, pl.ds(0, V - 1)], C + p)
        mk("sumC")
        val = recv_c[p, 0].astype(F32)
        for v in range(1, V):
            val = val + recv_c[p, v].astype(F32)
        low_u = (val * inv_root).astype(BF16)
        recv_u[p, my_q] = low_u

        def tell_update():
            for v in all_var:
                send(recv_u.at[p, my_q], recv_u.at[p, my_q], U + p, v, ms, UQ + p * O + my_q)

        def tell_sums():
            upd = low_u.astype(F32)
            now = cur[:, pl.ds(pl.multiple_of(my_q * chunk, chunk), chunk)]
            cross = jnp.sum(now * upd, axis=1, keepdims=True)
            square = jnp.sum(upd * upd, axis=1, keepdims=True)
            both = jnp.where(lane == sub, cross, jnp.where(lane == sub + ph, square, 0.0))
            slot = ms * O + my_q
            recv_s[p, slot] = jnp.sum(both, axis=0, keepdims=True)
            for s in samps + [ms]:
                for v in all_var:
                    send(recv_s.at[p, slot], recv_s.at[p, slot], SM + p, v, s)
            for s in samps:
                send(recv_s.at[p, slot], recv_s.at[p, slot], SM + p, mv, s)

        if p + 1 < PASSES:
            tell_update()
            tell_sums()
        else:
            tell_sums()
            tell_update()
        mk(None)

    turned = 2 * LANES

    def turn_rows(i, c):
        at = pl.ds(pl.multiple_of(i * turned, turned), turned)
        for j in range(width // turned):
            cut = slice(j * turned, (j + 1) * turned)
            xt_ref[cut, at] = x_ref[at, cut].T
        return c

    pl.when(serves)(own_slots)
    factors = []
    for p in range(PASSES):
        mk("gather")
        send_gradient(p)
        mk("mid")
        if p == 0:
            for s in samps:
                send(recv_p.at[ms], recv_p.at[ms], SC, mv, s)
            mk("turn")
            lax.fori_loop(0, rows // turned, turn_rows, 0)
            mk("mid")
        if p == 1:
            got(recv_p.at[pl.ds(0, S - 1)], SC)
            val = recv_p[0]
            for s in range(1, S):
                val = val + recv_p[s]
            scores_out[...] = val * inv_root
        if p > 0:
            factors.append(length(p - 1))
        factor = factors[-1] if p else None
        mk(None)
        pl.when(serves)(functools.partial(serve, p, factor))
        mk("adv")
        if p > 0:
            advance(factor, p - 1, cur)
        mk("waitB")
        pl.when(serves)(lambda: got(recv_b.at[p, pl.ds(0, V - 1)], B + p))
        unless(serves, lambda: got(recv_b.at[p], B + p))
        mk("spread")
        way = jnp.concatenate([recv_b[p, g] for g in range(V)], axis=1).astype(F32)
        which = high_t[...]
        wide = jnp.concatenate([jnp.where(which == float(t), way, 0.0) for t in range(tiles)], axis=0)
        found = dot(wide.astype(BF16), low[...], NT).astype(BF16)
        for t in range(tiles):
            d_held[:, t * LANES:(t + 1) * LANES] = found[t * ph:(t + 1) * ph]
        mk("upd")

        for k, (v, q) in enumerate(owners):
            at = pl.ds(pl.multiple_of(q * chunk, chunk), chunk)
            send_c[p, q] = dot(d_held[...], xt_ref[:, at]).astype(BF16)
            if k < O - 1:
                send(send_c.at[p, q], recv_c.at[p, mv], C + p, v, ms)
            else:
                def away(q=q, v=v):
                    send(send_c.at[p, q], recv_c.at[p, mv], C + p, v, ms)

                other_only(away)

                def stay(q=q):
                    recv_c[p, mv] = send_c[p, q]

                owner_only(stay)
        mk(None)
        owner_only(functools.partial(reduce, p))
        mk("waitU")
        for k, (v, q) in enumerate(reversed(owners)):
            def arrive(q=q):
                got(recv_u.at[p, q], UQ + p * O + q)

            if k == 0:
                other_only(arrive)
            else:
                arrive()
            if p + 1 < PASSES:
                at = pl.ds(pl.multiple_of(q * chunk, chunk), chunk)
                new = dot(recv_u[p, q], x_ref[at, :])
                if k == 0:
                    part[...] = new
                else:
                    part[...] += new

    mk("fin")
    factors.append(length(PASSES - 1))
    factor = factors[-1]
    advance(factor, PASSES - 1, resid_out)

    coef_out[...] = jnp.zeros((ph, fit), F32)
    coef_out[:, 0:kept] = beta_v[...]
    val = coef_out[...]
    for p in range(PASSES):
        unless(keeps, functools.partial(lambda p: got(recv_d.at[p], D + p), p))
        val = val + factors[p] * recv_d[p].astype(F32)
    coef_out[...] = val
    mk("drain")

    sent(ids_all.at[pl.ds(0, V - 1)], IDS)
    sent(recv_p.at[pl.ds(0, S - 1)], SC)

    def drain_a(p):
        pl.when(serves)(lambda: sent(recv_a.at[p, pl.ds(0, V - 1)], A + p))
        unless(serves, lambda: sent(recv_a.at[p, pl.ds(0, V)], A + p))

    def drain_serve():
        for p in range(PASSES):
            sent(recv_a.at[p, pl.ds(0, N - 1)], B + p)
            pl.when(keeps)(functools.partial(lambda p: sent(blank.at[pl.ds(0, S - 1)], D + p), p))
            unless(keeps, functools.partial(lambda p: sent(blank, D + p), p))

    def drain_owner():
        for p in range(PASSES):
            sent(send_c.at[p, pl.ds(0, O - 1)], C + p)
            sent(recv_c.at[p, pl.ds(0, V - 1)], U + p)
            sent(recv_s.at[p, pl.ds(0, N - 1)], SM + p)

    def drain_other():
        for p in range(PASSES):
            sent(send_c.at[p], C + p)

    def drain_gives():
        sent(beta_v, BETA)
        sent(inv.at[0], INV)

    for p in range(PASSES):
        drain_a(p)
    pl.when(serves)(drain_serve)
    owner_only(drain_owner)
    pl.when(gives)(drain_gives)
    other_only(drain_other)


def on_device(geno, scale_index, scale_table, residual, beta_active, block_inverse, active_ids, admit_ids):
    V, S = lax.axis_size("var"), lax.axis_size("samp")
    N = V * S
    O = V // 4
    assert V % 8 == 0 and S >= 4
    rows, width = geno.shape
    ph = residual.shape[0]
    fit = active_ids.shape[0] + admit_ids.shape[0]
    pad = LANES * pl.cdiv(2 * fit // V, LANES)
    chunk = rows // O
    vmem = pl.BlockSpec(memory_space=pltpu.VMEM)
    hbm = pl.BlockSpec(memory_space=pl.ANY)
    n_send = 4 + 6 * PASSES
    n_recv = n_send + PASSES * O
    per_group = rows // scale_index.shape[0]
    out = pl.pallas_call(
        functools.partial(kernel, V, S, pad),
        out_shape=(pltpu.VMEM((ph, width), F32), pltpu.VMEM((ph, fit), F32), pltpu.VMEM((ph, rows), F32)),
        in_specs=[hbm] * 8,
        out_specs=(vmem, vmem, vmem),
        scratch_shapes=[
            pltpu.VMEM((rows, width), BF16),
            pltpu.VMEM((width, rows), BF16),
            pltpu.VMEM(scale_index.shape, jnp.int32),
            pltpu.SMEM(scale_table.shape, F32),
            pltpu.VMEM((ph, rows), F32),
            pltpu.VMEM(beta_active.shape, F32),
            pltpu.VMEM(block_inverse.shape, F32),
            pltpu.VMEM((1, active_ids.shape[0]), jnp.int32),
            pltpu.VMEM((1, admit_ids.shape[0]), jnp.int32),
            pltpu.VMEM(scale_index.shape, F32),
            pltpu.VMEM((ph, rows), BF16),
            pltpu.VMEM((ph, width), F32),
            pltpu.VMEM((LANES, V * pad), BF16),
            pltpu.VMEM((ph, V * pad), F32),
            pltpu.VMEM((V, fit), F32),
            pltpu.VMEM((pad, fit), BF16),
            pltpu.VMEM((fit, fit), BF16),
            pltpu.VMEM((2,) + block_inverse.shape, BF16),
            pltpu.VMEM(beta_active.shape, F32),
            pltpu.VMEM((V, 1, fit), jnp.int32),
            pltpu.VMEM((S, ph, fit), BF16),
            pltpu.VMEM((ph, width), BF16),
            pltpu.VMEM((ph, fit), F32),
            pltpu.VMEM((ph, fit), F32),
            pltpu.VMEM((PASSES, ph, fit), BF16),
            pltpu.VMEM((PASSES, V, ph, pad), BF16),
            pltpu.VMEM((PASSES, N, ph, pad), BF16),
            pltpu.VMEM((PASSES, V, ph, pad), BF16),
            pltpu.VMEM((PASSES, V, ph, pad), BF16),
            pltpu.VMEM((PASSES, O, ph, chunk), BF16),
            pltpu.VMEM((PASSES, V, ph, chunk), BF16),
            pltpu.VMEM((PASSES, O, ph, chunk), BF16),
            pltpu.VMEM((S, ph, width), F32),
            pltpu.VMEM((PASSES, N, 1, LANES), F32),
            pltpu.VMEM((PASSES, ph, fit), BF16),
            pltpu.SemaphoreType.DMA((rows // (2 * per_group),)),
            pltpu.SemaphoreType.DMA((7,)),
            pltpu.SemaphoreType.DMA((n_send,)),
            pltpu.SemaphoreType.DMA((n_recv,)),
        ],
        compiler_params=pltpu.CompilerParams(
            collective_id=0, has_side_effects=True, vmem_limit_bytes=60 * 1024 * 1024
        ),
    )(geno, scale_index, scale_table, residual, beta_active, block_inverse, active_ids[None], admit_ids[None])

    def hand_out(*refs):
        half = len(refs) // 2
        for a, b in zip(refs[:half], refs[half:]):
            b[...] = a[...]

    return pl.pallas_call(
        hand_out, out_shape=tuple(jax.ShapeDtypeStruct(o.shape, o.dtype) for o in out),
        in_specs=[vmem] * 3, out_specs=(vmem,) * 3,
        compiler_params=pltpu.CompilerParams(vmem_limit_bytes=1024 * 1024),
    )(*out)


def solution(mesh):
    placed = (
        P("samp", "var"), P("samp", "var"), P(), P(None, "samp"), P(None, "var"),
        P("var", None, None), P("var"), P("var"),
    )
    return jax.shard_map(
        on_device, mesh=mesh, in_specs=placed,
        out_specs=(P(None, "var"), P(None, "var"), P(None, "samp")), check_vma=False,
    )
```

time: 66.1 us -> 58.9 us (0.89)
  Pallas kernels: 65.3 us -> 58.1 us
    pallas_call x1, Pallas kernels: 64.6 us -> 57.5 us  [on_device(): pl.pallas_call(functools.partial(kernel, V, S, pad), out_shape=(pltpu.VME...]
where the time goes in v3:
time: 58.9 us; the launch traced here: 58.8 us
  Pallas kernels  58.1 us (99%)
  between operations  0.64 us (1%)
    pallas_call x1, Pallas kernels, on_device(): pl.pallas_call(functools.partial(kernel, V, S, pad), out_shape=(pltpu.VME...  57.5 us

profile of v3, /device:TPU:0, one launch (start us, length us, event | category | flops | bytes accessed | tf_op | source)
XLA Modules:
  0.0 58.8 jit_solution(16822565065581750051)
XLA Ops:
  0.6 57.5 %shard_map.103 = (f32[8,2048]{1,0:T(8,128)S(1)}, f32[8,512]{1,0:T(8,128)S(1)}, f32[8,2048]{1,0:T(8,128)S(1)}) custom-call(bf16[2048,2048]{1,0:T(8,128)(2,1)} %geno.1, s32[16,2048]{1,0:T(8,128)} %sidx.1, f32[16]{0:T(128)} %table.1, f32[8,2048]{1,0:T(8,128)} %resid.1, f32[8,448]{1,0:T(8,128)} %beta.1, f32[2,256,256]{2,1,0:T(8,128)} %binv.1, s32[1,448]{1,0:T(1,128)} %bitcast.2, ...), custom_call_target="tpu_custom_call" | custom-call | tf_op jit(solution)/shard_map/pallas_call | solution.py:552
  58.1 0.7 %shard_map.104 = (f32[8,2048]{1,0:T(8,128)}, f32[8,512]{1,0:T(8,128)}, f32[8,2048]{1,0:T(8,128)}) custom-call(f32[8,2048]{1,0:T(8,128)S(1)} %get-tuple-element.6.refs_0_, f32[8,512]{1,0:T(8,128)S(1)} %get-tuple-element.7.refs_1_, f32[8,2048]{1,0:T(8,128)S(1)} %get-tuple-element.8.refs_2_), custom_call_target="tpu_custom_call" | custom-call | tf_op jit(solution)/shard_map/pallas_call | solution.py:608

commit v4 on v3

--- a/solution.py
+++ b/solution.py
@@ -61,9 +61,6 @@
     tiles = width // LANES
     piece = 2 * per_group
     n_loads = rows // piece
-    per_step = 2 if n_loads % 2 == 0 else 1
-    step = per_step * piece
-    n_steps = rows // step
     inv_root = 1.0 / math.sqrt(rows * S)
     mv, ms = lax.axis_index("var"), lax.axis_index("samp")
     me = ms * V + mv
@@ -71,27 +68,9 @@
     mk("greet")
     barrier = pltpu.get_barrier_semaphore()
 
-    samps = [lax.rem(ms + d, S) for d in range(1, S)] + [ms]
+    samps = [lax.rem(ms + d, S) for d in range(1, S)]
     if S == 4:
-        samps = [3 - ms] + [ms + d - 2 * d * lax.rem(lax.div(ms, d), 2) for d in (2, 1)] + [ms]
-    others = [lax.rem(mv + d, V) for d in range(V - 1, -1, -1)]
-    for s in samps:
-        for v in others[:-1] if s is ms else others:
-            pl.semaphore_signal(
-                barrier, inc=1, device_id={"var": v, "samp": s}, device_id_type=pl.DeviceIdType.MESH
-            )
-    mk("start")
-
-    def load(i):
-        at = pl.ds(pl.multiple_of(i * piece, piece), piece)
-        return pltpu.make_async_copy(geno.at[at], x_ref.at[at], load_sem.at[i])
-
-    small = [(table, table_s), (sidx, sidx_v), (resid, cur), (active, act_v), (admit, adm_v), (beta, beta_v), (binv, binv_v)]
-    pulls = [pltpu.make_async_copy(a, b, in_sem.at[i]) for i, (a, b) in enumerate(small)]
-    for c in pulls[:5]:
-        c.start()
-    load(0).start()
-    load(1).start()
+        samps = [3 - ms] + [ms + d - 2 * d * lax.rem(lax.div(ms, d), 2) for d in (2, 1)]
 
     h, z, c0 = lax.div(mv, 8), lax.rem(lax.div(mv, 2), 4), lax.rem(mv, 2)
     side = lax.div(z, 2)
@@ -109,7 +88,44 @@
     z0 = z + side * (3 - 2 * z)
     zs = [side * 3 + (1 - 2 * side) * k for k in (3, 2, 1 - z0, z0)]
     all_var = [8 * hh + 2 * zz + cc for hh in hs for zz in zs for cc in (1 - c0, c0)][:-1]
-    samps = samps[:-1]
+
+    def hello(v, s):
+        pl.semaphore_signal(
+            barrier, inc=1, device_id={"var": v, "samp": s}, device_id_type=pl.DeviceIdType.MESH
+        )
+
+    for v in all_var:
+        hello(v, ms)
+    for s in samps:
+        hello(mv, s)
+
+    def greet_all():
+        for s in samps:
+            for v in all_var:
+                hello(v, s)
+
+    pl.when(is_owner)(greet_all)
+
+    def greet_owners():
+        for s in samps:
+            for v, _ in owners:
+                hello(v, s)
+
+    pl.when(jnp.logical_not(is_owner))(greet_owners)
+    mk("start")
+
+    def load(i):
+        at = pl.ds(pl.multiple_of(i * piece, piece), piece)
+        return pltpu.make_async_copy(geno.at[at], x_ref.at[at], load_sem.at[i])
+
+    small = [(table, table_s), (sidx, sidx_v), (resid, cur), (active, act_v), (admit, adm_v), (beta, beta_v), (binv, binv_v)]
+    pulls = [pltpu.make_async_copy(a, b, in_sem.at[i]) for i, (a, b) in enumerate(small)]
+    for c in pulls[:5]:
+        c.start()
+    load(0).start()
+    for c in pulls[5:]:
+        c.start()
+
 
     def owner_only(fn):
         pl.when(is_owner)(fn)
@@ -141,6 +157,7 @@
     D = SM + PASSES
     U = D + PASSES
     UQ = U + PASSES
+    IQ = UQ + PASSES * O
 
     tri[...] = jnp.where(
         lax.broadcasted_iota(jnp.int32, (fit, fit), 0) < lax.broadcasted_iota(jnp.int32, (fit, fit), 1),
@@ -151,10 +168,7 @@
     for c in pulls[:5]:
         c.wait()
     mk("setup")
-    for i in range(2, n_loads):
-        if i == n_loads // 2:
-            for c in pulls[5:]:
-                c.start()
+    for i in range(1, n_loads):
         load(i).start()
     ids_all[mv, :, 0:kept] = act_v[...]
     ids_all[mv, :, kept:fit] = adm_v[...]
@@ -166,34 +180,32 @@
     rlow[...] = cur[...].astype(BF16)
     cols = 256
 
-    def screen(i, c):
-        for k in range(per_step):
-            load(i * per_step + k).wait()
-        at = pl.ds(pl.multiple_of(i * step, step), step)
+    def screen(begin, n_pieces):
+        for k in range(n_pieces):
+            load(begin + k).wait()
+        size = n_pieces * piece
+        start = begin * piece
+        at = pl.ds(pl.multiple_of(start, piece), size)
         left = rlow[:, at]
         for j in range(width // cols):
             lane = slice(j * cols, (j + 1) * cols)
             block = []
-            for n in range(step // per_group):
-                sub = pl.ds(pl.multiple_of(i * step + n * per_group, per_group), per_group)
-                scale = scale_ref[pl.ds(i * (step // per_group) + n, 1), lane]
+            for n in range(size // per_group):
+                sub = pl.ds(pl.multiple_of(start + n * per_group, per_group), per_group)
+                scale = scale_ref[pl.ds(begin * (piece // per_group) + n, 1), lane]
                 block.append(x_ref[sub, lane].astype(F32) * scale)
             block = jnp.concatenate(block, axis=0).astype(BF16)
             x_ref[at, lane] = block
             part[:, lane] += dot(left, block)
-        return c
-
-    first = pl.cdiv(n_steps, 4)
+
     mk("screen1")
-    lax.fori_loop(0, first, screen, 0)
+    screen(0, 1)
     mk("barrier")
-    pl.semaphore_wait(barrier, N - 1)
+    pl.when(is_owner)(lambda: pl.semaphore_wait(barrier, N - 1))
+    pl.when(jnp.logical_not(is_owner))(lambda: pl.semaphore_wait(barrier, V - 1 + (S - 1) * (1 + O)))
     for v in all_var:
-        send(ids_all.at[mv], ids_all.at[mv], IDS, v, ms)
-
-    mk("screen2")
-    lax.fori_loop(first, n_steps, screen, 0)
-    recv_p[ms] = part[...]
+        send(ids_all.at[mv], ids_all.at[mv], IDS, v, ms, IQ + my_q)
+
     mk("inv")
     for c in pulls[5:]:
         c.wait()
@@ -211,37 +223,44 @@
         inv[1] = inv[0]
 
     pl.when(keeps)(keep)
-    mk("idswait")
-    got(ids_all.at[pl.ds(0, V - 1)], IDS)
-    mk("idsproc")
+    mk("screen2")
+    pairs = (n_loads - 1) // 2
+
+    def two(i, c):
+        screen(1 + 2 * i, 2)
+        return c
+
+    lax.fori_loop(0, pairs, two, 0)
+    if 1 + 2 * pairs < n_loads:
+        screen(n_loads - 1, 1)
+    recv_p[ms] = part[...]
     line = lax.broadcasted_iota(jnp.int32, (V, fit), 0)
-
-    def lines(g):
-        return ids_all[g, 0:1, :]
-
-    all_ids = jnp.zeros((V, fit), jnp.int32)
-    for g in range(V):
-        all_ids = jnp.where(line == g, lines(g), all_ids)
-    column = all_ids - mv * width
-    held = (column >= 0) & (column < width)
-    serial = dot(jnp.where(held, 1.0, 0.0).astype(BF16), tri[...])
-    serial = jnp.where(held, serial, -1.0)
-    column = jnp.where(held, column, 0)
     eight = lax.broadcasted_iota(jnp.int32, (8, fit), 0)
     turn = lax.broadcasted_iota(jnp.int32, (pad, fit), 0).astype(F32)
     lane_no = lax.broadcasted_iota(jnp.int32, (LANES, pad), 0).astype(F32)
-    for g in range(V):
-        col = column[g:g + 1]
-        digits = jnp.where(
-            eight == 0, lax.shift_right_logical(col, 7),
-            jnp.where(eight == 1, col & 127, jnp.where(eight == 2, 1, 0)),
-        ).astype(F32).astype(BF16)
-        place = jnp.where(turn == serial[g:g + 1], 1.0, 0.0).astype(BF16)
-        found = dot(digits, place, NT)
-        here = found[2:3] > 0.5
-        at = slice(g * pad, (g + 1) * pad)
-        high_t[:, at] = jnp.broadcast_to(jnp.where(here, found[0:1], -1.0), (ph, pad))
-        low[:, at] = jnp.where(lane_no == jnp.where(here, found[1:2], -1.0), 1.0, 0.0).astype(BF16)
+
+    def place_half(hh, ss):
+        first_g = 8 * hh + 4 * ss
+        column = jnp.zeros((8, fit), jnp.int32)
+        for i in range(4):
+            column = jnp.where(eight == i, ids_all[first_g + i], column)
+        column = column - mv * width
+        held = (column >= 0) & (column < width)
+        serial = dot(jnp.where(held, 1.0, 0.0).astype(BF16), tri[...])
+        serial = jnp.where(held, serial, -1.0)
+        column = jnp.where(held, column, 0)
+        for i in range(4):
+            col = column[i:i + 1]
+            digits = jnp.where(
+                eight == 0, lax.shift_right_logical(col, 7),
+                jnp.where(eight == 1, col & 127, jnp.where(eight == 2, 1, 0)),
+            ).astype(F32).astype(BF16)
+            place = jnp.where(turn == serial[i:i + 1], 1.0, 0.0).astype(BF16)
+            found = dot(digits, place, NT)
+            here = found[2:3] > 0.5
+            at = pl.ds(pl.multiple_of((first_g + i) * pad, pad), pad)
+            high_t[:, at] = jnp.broadcast_to(jnp.where(here, found[0:1], -1.0), (ph, pad))
+            low[:, at] = jnp.where(lane_no == jnp.where(here, found[1:2], -1.0), 1.0, 0.0).astype(BF16)
 
     mk(None)
 
@@ -354,6 +373,9 @@
         for s in samps:
             send(send_b.at[p, mv], recv_b.at[p, my_g], B + p, mv, s)
         recv_b[p, my_g] = send_b[p, mv]
+        mk(None)
+
+    def tell_direct(p):
         for s in samps:
             send(direct.at[p], recv_d.at[p], D + p, my_g, s)
 
@@ -366,7 +388,6 @@
             recv_d[p] = direct[p]
 
         pl.when(keeps)(stay)
-        mk(None)
 
     def reduce(p):
         mk("gotC")
@@ -413,15 +434,20 @@
             xt_ref[cut, at] = x_ref[at, cut].T
         return c
 
-    pl.when(serves)(own_slots)
+    for n, (hh, ss) in enumerate(reversed(halves)):
+        mk("idswait")
+        got(ids_all.at[pl.ds(0, 3 if n == 0 else 4)], IQ + 2 * hh + ss)
+        mk("idsproc")
+        place_half(hh, ss)
+        mk(None)
+        if n == 0:
+            pl.when(serves)(own_slots)
     factors = []
     for p in range(PASSES):
         mk("gather")
         send_gradient(p)
         mk("mid")
         if p == 0:
-            for s in samps:
-                send(recv_p.at[ms], recv_p.at[ms], SC, mv, s)
             mk("turn")
             lax.fori_loop(0, rows // turned, turn_rows, 0)
             mk("mid")
@@ -466,6 +492,10 @@
                     recv_c[p, mv] = send_c[p, q]
 
                 owner_only(stay)
+        pl.when(serves)(functools.partial(tell_direct, p))
+        if p == 0:
+            for s in samps:
+                send(recv_p.at[ms], recv_p.at[ms], SC, mv, s)
         mk(None)
         owner_only(functools.partial(reduce, p))
         mk("waitU")
@@ -547,7 +577,7 @@
     vmem = pl.BlockSpec(memory_space=pltpu.VMEM)
     hbm = pl.BlockSpec(memory_space=pl.ANY)
     n_send = 4 + 6 * PASSES
-    n_recv = n_send + PASSES * O
+    n_recv = n_send + PASSES * O + O
     per_group = rows // scale_index.shape[0]
     out = pl.pallas_call(
         functools.partial(kernel, V, S, pad),

time: 58.9 us -> 57.7 us (0.980)
  Pallas kernels: 58.1 us -> 56.9 us
    pallas_call x1, Pallas kernels: 57.5 us -> 56.3 us  [on_device(): pl.pallas_call(functools.partial(kernel, V, S, pad), out_shape=(pltpu.VME...]
where the time goes in v4:
time: 57.7 us; the launch traced here: 57.6 us
  Pallas kernels  56.9 us (99%)
  between operations  0.64 us (1%)
    pallas_call x1, Pallas kernels, on_device(): pl.pallas_call(functools.partial(kernel, V, S, pad), out_shape=(pltpu.VME...  56.3 us

profile of v4, /device:TPU:0, one launch (start us, length us, event | category | flops | bytes accessed | tf_op | source)
XLA Modules:
  0.0 57.6 jit_solution(2153111382297946906)
XLA Ops:
  0.6 56.3 %shard_map.103 = (f32[8,2048]{1,0:T(8,128)S(1)}, f32[8,512]{1,0:T(8,128)S(1)}, f32[8,2048]{1,0:T(8,128)S(1)}) custom-call(bf16[2048,2048]{1,0:T(8,128)(2,1)} %geno.1, s32[16,2048]{1,0:T(8,128)} %sidx.1, f32[16]{0:T(128)} %table.1, f32[8,2048]{1,0:T(8,128)} %resid.1, f32[8,448]{1,0:T(8,128)} %beta.1, f32[2,256,256]{2,1,0:T(8,128)} %binv.1, s32[1,448]{1,0:T(1,128)} %bitcast.2, ...), custom_call_target="tpu_custom_call" | custom-call | tf_op jit(solution)/shard_map/pallas_call | solution.py:582
  56.9 0.7 %shard_map.104 = (f32[8,2048]{1,0:T(8,128)}, f32[8,512]{1,0:T(8,128)}, f32[8,2048]{1,0:T(8,128)}) custom-call(f32[8,2048]{1,0:T(8,128)S(1)} %get-tuple-element.6.refs_0_, f32[8,512]{1,0:T(8,128)S(1)} %get-tuple-element.7.refs_1_, f32[8,2048]{1,0:T(8,128)S(1)} %get-tuple-element.8.refs_2_), custom_call_target="tpu_custom_call" | custom-call | tf_op jit(solution)/shard_map/pallas_call | solution.py:638

commit v5 on v4

--- a/solution.py
+++ b/solution.py
@@ -9,6 +9,7 @@
 from jax.sharding import PartitionSpec as P
 
 PASSES = 3
+SHARES = (0, 1, 3, 4, 7, 8)
 PENALTY = 0.5
 EPSILON = 1e-06
 LANES = 128
@@ -36,7 +37,7 @@
     V, S, pad,
     geno, sidx, table, resid, beta, binv, active, admit,
     scores_out, coef_out, resid_out,
-    x_ref, xt_ref, sidx_v, table_s, cur, beta_v, binv_v, act_v, adm_v,
+    x_ref, xt_ref, pick, xc_ref, xct_ref, part_c, sidx_v, table_s, cur, beta_v, binv_v, act_v, adm_v,
     scale_ref, rlow, part, low, high_t, marks_v, place_v, tri, inv, beta_two, ids_all, blank,
     d_held, coef, grad, direct,
     send_a, recv_a, send_b, recv_b, send_c, recv_c, recv_u, recv_p, recv_s, recv_d,
@@ -274,19 +275,46 @@
         marks_v[...] = marks
         mk(None)
 
+    marks_at = [c * n_loads // 8 for c in SHARES]
+
+    def build_pick():
+        for t in range(tiles):
+            one = jnp.where(high_t[0:1, :] == float(t), low[...].astype(F32), 0.0)
+            pick[t * LANES:(t + 1) * LANES, :] = one.astype(BF16)
+
+    def compact_piece(i, c):
+        at = pl.ds(pl.multiple_of(i * piece, piece), piece)
+        block = dot(x_ref[at, :], pick[...]).astype(BF16)
+        xc_ref[at, :] = block
+        for j in range(V * pad // turned):
+            cut = slice(j * turned, (j + 1) * turned)
+            xct_ref[cut, at] = xc_ref[at, cut].T
+        return c
+
+    def compact(k):
+        lax.fori_loop(marks_at[k], marks_at[k + 1], compact_piece, 0)
+
+    turned = 2 * LANES
+
     def send_gradient(p):
-        wide = jnp.concatenate([part[:, t * LANES:(t + 1) * LANES] for t in range(tiles)], axis=0).astype(BF16)
+        done = p == PASSES - 1
+        if done:
+            for g in range(V):
+                send_a[p, g] = part_c[:, g * pad:(g + 1) * pad].astype(BF16)
+        else:
+            wide = jnp.concatenate([part[:, t * LANES:(t + 1) * LANES] for t in range(tiles)], axis=0).astype(BF16)
         for n, (hh, ss) in enumerate(halves):
             base = 8 * hh + 4 * ss
-            at = pl.ds(pl.multiple_of(base * pad, 4 * pad), 4 * pad)
-            found = dot(wide, low[:, at])
-            which = high_t[:, at]
-            out = jnp.zeros((ph, 4 * pad), F32)
-            for t in range(tiles):
-                out = jnp.where(which == float(t), found[t * ph:(t + 1) * ph], out)
-            out = out.astype(BF16)
-            for k in range(4):
-                send_a[p, base + k] = out[:, k * pad:(k + 1) * pad]
+            if not done:
+                at = pl.ds(pl.multiple_of(base * pad, 4 * pad), 4 * pad)
+                found = dot(wide, low[:, at])
+                which = high_t[:, at]
+                out = jnp.zeros((ph, 4 * pad), F32)
+                for t in range(tiles):
+                    out = jnp.where(which == float(t), found[t * ph:(t + 1) * ph], out)
+                out = out.astype(BF16)
+                for k in range(4):
+                    send_a[p, base + k] = out[:, k * pad:(k + 1) * pad]
             v = 8 * hh + 2 * (1 + ss) + 1
             last = n == len(halves) - 1
             turns = [lax.rem(ms + d, 4) for d in (2, 3, 1)]
@@ -425,8 +453,6 @@
             tell_update()
         mk(None)
 
-    turned = 2 * LANES
-
     def turn_rows(i, c):
         at = pl.ds(pl.multiple_of(i * turned, turned), turned)
         for j in range(width // turned):
@@ -452,6 +478,9 @@
             lax.fori_loop(0, rows // turned, turn_rows, 0)
             mk("mid")
         if p == 1:
+            mk("cmpA1")
+            compact(3)
+            mk("mid")
             got(recv_p.at[pl.ds(0, S - 1)], SC)
             val = recv_p[0]
             for s in range(1, S):
@@ -465,21 +494,31 @@
         mk("adv")
         if p > 0:
             advance(factor, p - 1, cur)
+        if p < 2:
+            mk("cmpB")
+            if p == 0:
+                build_pick()
+            compact(0 if p == 0 else 4)
         mk("waitB")
         pl.when(serves)(lambda: got(recv_b.at[p, pl.ds(0, V - 1)], B + p))
         unless(serves, lambda: got(recv_b.at[p], B + p))
         mk("spread")
-        way = jnp.concatenate([recv_b[p, g] for g in range(V)], axis=1).astype(F32)
-        which = high_t[...]
-        wide = jnp.concatenate([jnp.where(which == float(t), way, 0.0) for t in range(tiles)], axis=0)
-        found = dot(wide.astype(BF16), low[...], NT).astype(BF16)
-        for t in range(tiles):
-            d_held[:, t * LANES:(t + 1) * LANES] = found[t * ph:(t + 1) * ph]
+        way = jnp.concatenate([recv_b[p, g] for g in range(V)], axis=1)
+        if p == 0:
+            way = way.astype(F32)
+            which = high_t[...]
+            wide = jnp.concatenate([jnp.where(which == float(t), way, 0.0) for t in range(tiles)], axis=0)
+            found = dot(wide.astype(BF16), low[...], NT).astype(BF16)
+            for t in range(tiles):
+                d_held[:, t * LANES:(t + 1) * LANES] = found[t * ph:(t + 1) * ph]
         mk("upd")
 
         for k, (v, q) in enumerate(owners):
             at = pl.ds(pl.multiple_of(q * chunk, chunk), chunk)
-            send_c[p, q] = dot(d_held[...], xt_ref[:, at]).astype(BF16)
+            if p == 0:
+                send_c[p, q] = dot(d_held[...], xt_ref[:, at]).astype(BF16)
+            else:
+                send_c[p, q] = dot(way, xct_ref[:, at]).astype(BF16)
             if k < O - 1:
                 send(send_c.at[p, q], recv_c.at[p, mv], C + p, v, ms)
             else:
@@ -497,7 +536,14 @@
             for s in samps:
                 send(recv_p.at[ms], recv_p.at[ms], SC, mv, s)
         mk(None)
+        if p == 0:
+            mk("cmpC")
+            compact(1)
+            mk(None)
         owner_only(functools.partial(reduce, p))
+        if p == 0:
+            mk("cmpU")
+            compact(2)
         mk("waitU")
         for k, (v, q) in enumerate(reversed(owners)):
             def arrive(q=q):
@@ -509,11 +555,13 @@
                 arrive()
             if p + 1 < PASSES:
                 at = pl.ds(pl.multiple_of(q * chunk, chunk), chunk)
-                new = dot(recv_u[p, q], x_ref[at, :])
+                left = PASSES - 2 - p
+                new = dot(recv_u[p, q], x_ref[at, :] if left else xc_ref[at, :])
+                total = part if left else part_c
                 if k == 0:
-                    part[...] = new
+                    total[...] = new
                 else:
-                    part[...] += new
+                    total[...] += new
 
     mk("fin")
     factors.append(length(PASSES - 1))
@@ -587,6 +635,10 @@
         scratch_shapes=[
             pltpu.VMEM((rows, width), BF16),
             pltpu.VMEM((width, rows), BF16),
+            pltpu.VMEM((width, V * pad), BF16),
+            pltpu.VMEM((rows, V * pad), BF16),
+            pltpu.VMEM((V * pad, rows), BF16),
+            pltpu.VMEM((ph, V * pad), F32),
             pltpu.VMEM(scale_index.shape, jnp.int32),
             pltpu.SMEM(scale_table.shape, F32),
             pltpu.VMEM((ph, rows), F32),

time: 57.7 us -> 56 us (0.971)
  Pallas kernels: 56.9 us -> 55.2 us
    pallas_call x1, Pallas kernels: 56.3 us -> 54.6 us  [on_device(): pl.pallas_call(functools.partial(kernel, V, S, pad), out_shape=(pltpu.VME...]
where the time goes in v5:
time: 56 us; the launch traced here: 55.9 us
  Pallas kernels  55.2 us (99%)
  between operations  0.64 us (1%)
    pallas_call x1, Pallas kernels, on_device(): pl.pallas_call(functools.partial(kernel, V, S, pad), out_shape=(pltpu.VME...  54.6 us

profile of v5, /device:TPU:0, one launch (start us, length us, event | category | flops | bytes accessed | tf_op | source)
XLA Modules:
  0.0 55.9 jit_solution(12757998561839953392)
XLA Ops:
  0.6 54.6 %shard_map.103 = (f32[8,2048]{1,0:T(8,128)S(1)}, f32[8,512]{1,0:T(8,128)S(1)}, f32[8,2048]{1,0:T(8,128)S(1)}) custom-call(bf16[2048,2048]{1,0:T(8,128)(2,1)} %geno.1, s32[16,2048]{1,0:T(8,128)} %sidx.1, f32[16]{0:T(128)} %table.1, f32[8,2048]{1,0:T(8,128)} %resid.1, f32[8,448]{1,0:T(8,128)} %beta.1, f32[2,256,256]{2,1,0:T(8,128)} %binv.1, s32[1,448]{1,0:T(1,128)} %bitcast.2, ...), custom_call_target="tpu_custom_call" | custom-call | tf_op jit(solution)/shard_map/pallas_call | solution.py:630
  55.2 0.7 %shard_map.104 = (f32[8,2048]{1,0:T(8,128)}, f32[8,512]{1,0:T(8,128)}, f32[8,2048]{1,0:T(8,128)}) custom-call(f32[8,2048]{1,0:T(8,128)S(1)} %get-tuple-element.6.refs_0_, f32[8,512]{1,0:T(8,128)S(1)} %get-tuple-element.7.refs_1_, f32[8,2048]{1,0:T(8,128)S(1)} %get-tuple-element.8.refs_2_), custom_call_target="tpu_custom_call" | custom-call | tf_op jit(solution)/shard_map/pallas_call | solution.py:690

commit v6 on v5

--- a/solution.py
+++ b/solution.py
@@ -9,7 +9,7 @@
 from jax.sharding import PartitionSpec as P
 
 PASSES = 3
-SHARES = (0, 1, 3, 4, 7, 8)
+SHARES = (0, 1, 3, 4, 6, 8)
 PENALTY = 0.5
 EPSILON = 1e-06
 LANES = 128

time: 56 us -> 55.8 us (level)
  no operation moved by 1% of the time
where the time goes in v6:
time: 55.8 us; the launch traced here: 55.6 us
  Pallas kernels  55 us (99%)
  between operations  0.64 us (1%)
    pallas_call x1, Pallas kernels, on_device(): pl.pallas_call(functools.partial(kernel, V, S, pad), out_shape=(pltpu.VME...  54.3 us

profile of v6, /device:TPU:0, one launch (start us, length us, event | category | flops | bytes accessed | tf_op | source)
XLA Modules:
  0.0 55.6 jit_solution(508802847801781072)
XLA Ops:
  0.6 54.3 %shard_map.103 = (f32[8,2048]{1,0:T(8,128)S(1)}, f32[8,512]{1,0:T(8,128)S(1)}, f32[8,2048]{1,0:T(8,128)S(1)}) custom-call(bf16[2048,2048]{1,0:T(8,128)(2,1)} %geno.1, s32[16,2048]{1,0:T(8,128)} %sidx.1, f32[16]{0:T(128)} %table.1, f32[8,2048]{1,0:T(8,128)} %resid.1, f32[8,448]{1,0:T(8,128)} %beta.1, f32[2,256,256]{2,1,0:T(8,128)} %binv.1, s32[1,448]{1,0:T(1,128)} %bitcast.2, ...), custom_call_target="tpu_custom_call" | custom-call | tf_op jit(solution)/shard_map/pallas_call | solution.py:630
  55.0 0.7 %shard_map.104 = (f32[8,2048]{1,0:T(8,128)}, f32[8,512]{1,0:T(8,128)}, f32[8,2048]{1,0:T(8,128)}) custom-call(f32[8,2048]{1,0:T(8,128)S(1)} %get-tuple-element.6.refs_0_, f32[8,512]{1,0:T(8,128)S(1)} %get-tuple-element.7.refs_1_, f32[8,2048]{1,0:T(8,128)S(1)} %get-tuple-element.8.refs_2_), custom_call_target="tpu_custom_call" | custom-call | tf_op jit(solution)/shard_map/pallas_call | solution.py:690
